TPU v7x, 8 devices: a whole 2x2x1 slice. The times are simulated.
8 devices in a mesh: data: 8 (over z, y, x, core).
Axes of the slice: x: 2, y: 2, z: 1, core: 2. Of those that a mesh axis runs over, the one named last changes fastest.
Arguments:
- x_now: bfloat16 [32, 784, 128], P('data')
- labels_now: int32 [32], P('data')
- x_next: bfloat16 [32, 784, 128], P('data')
- up_one: float32 [2, 128, 512], replicated
- down_one: float32 [2, 512, 128], replicated
- merge_proj: float32 [512, 512], replicated
- up_two: float32 [2, 512, 2048], replicated
- down_two: float32 [2, 2048, 512], replicated
- head_proj: float32 [512, 1000], replicated
- vel_up_one: float32 [2, 128, 512], replicated
- vel_down_one: float32 [2, 512, 128], replicated
- vel_merge_proj: float32 [512, 512], replicated
- vel_up_two: float32 [2, 512, 2048], replicated
- vel_down_two: float32 [2, 2048, 512], replicated
- vel_head_proj: float32 [512, 1000], replicated
Outputs:
- output 1: float32 [32, 1000], P('data')
- output 2: float32 [2, 128, 512], replicated
- output 3: float32 [2, 512, 128], replicated
- output 4: float32 [512, 512], replicated
- output 5: float32 [2, 512, 2048], replicated
- output 6: float32 [2, 2048, 512], replicated
- output 7: float32 [512, 1000], replicated
- output 8: float32 [2, 128, 512], replicated
- output 9: float32 [2, 512, 128], replicated
- output 10: float32 [512, 512], replicated
- output 11: float32 [2, 512, 2048], replicated
- output 12: float32 [2, 2048, 512], replicated
- output 13: float32 [512, 1000], replicated
All inputs are finite; a program needn't handle non-finite values.
Results may differ from a plain program's by a relative error of at most 0.0111885.
Values are sent between devices in bfloat16 or wider.
A program may use at most 1 GiB of HBM per device.

v0:
```python
import jax
import jax.numpy as jnp
from jax import lax
from jax.experimental import pallas as pl
from jax.experimental.pallas import tpu as pltpu
from jax.sharding import PartitionSpec as P

MOMENTUM = 0.9
TRUST = 0.1
LN_EPS = 1e-6
GELU_A = 0.7978845608028654
GELU_B = 0.044715 * GELU_A
F32 = jnp.float32
BF16 = jnp.bfloat16
VMEM_BYTES = 66_000_000

IMGS, TOKENS, WIDTH = 4, 784, 128
MERGED = TOKENS // 4
ROWS = IMGS * MERGED
WIDE = 4 * WIDTH
HID_ONE, HID_TWO = 4 * WIDTH, 4 * WIDE
CLASSES = 1000
TILE = 256
SHARD = 64
N_TILES = HID_TWO // TILE
FWD_TILE = 512


def dot_nn(a, b):
    return lax.dot_general(a, b, (((1,), (0,)), ((), ())), preferred_element_type=F32)


def dot_nt(a, b):
    return lax.dot_general(a, b, (((1,), (1,)), ((), ())), preferred_element_type=F32)


def dot_tn(a, b):
    return lax.dot_general(a, b, (((0,), (0,)), ((), ())), preferred_element_type=F32)


def norm_parts(vals):
    centered = vals - jnp.mean(vals, axis=-1, keepdims=True)
    variance = jnp.mean(centered * centered, axis=-1, keepdims=True)
    rstd = lax.rsqrt(variance + LN_EPS)
    return centered * rstd, rstd


def norm_back(grad, normed, rstd):
    mean_g = jnp.mean(grad, axis=-1, keepdims=True)
    mean_gn = jnp.mean(grad * normed, axis=-1, keepdims=True)
    return rstd * (grad - mean_g - normed * mean_gn)


def gelu_parts(pre):
    square = pre * pre
    half = 0.5 * jnp.tanh(pre * (GELU_A + GELU_B * square)) + 0.5
    return square, half


def gelu_slope(pre, square, half):
    return half * (1.0 + pre * (1.0 - half) * (2.0 * GELU_A + 6.0 * GELU_B * square))


def cast_rows(dst, src, rows, step):
    def body(i, carry):
        sl = pl.ds(pl.multiple_of(i * step, step), step)
        dst[sl, :] = src[sl, :].astype(BF16)
        return carry
    lax.fori_loop(0, rows // step, body, 0)


def lanes(index, size):
    return pl.ds(pl.multiple_of(index * size, size), size)


def permute_tokens(x_ref, x_f32, r0):
    x_f32[...] = x_ref[...].astype(F32)
    for j in range(4):
        r0[:, j * WIDTH:(j + 1) * WIDTH] = x_f32[pl.ds(j, ROWS, stride=4), :].astype(BF16)


def stage_one_block(resid, w_up, w_down):
    res_f = resid.astype(F32)
    normed = norm_parts(res_f)[0].astype(BF16)
    pre = dot_nn(normed, w_up)
    act = (pre * gelu_parts(pre)[1]).astype(BF16)
    return (res_f + dot_nn(act, w_down)).astype(BF16)


def stage_one_forward(r0, r1, r2, up_one, down_one):
    def body(j, carry):
        sl = lanes(j, WIDTH)
        mid = stage_one_block(r0[:, sl], up_one[0], down_one[0])
        r1[:, sl] = mid
        r2[:, sl] = stage_one_block(mid, up_one[1], down_one[1])
        return carry
    lax.fori_loop(0, 4, body, 0)


def stage_two_block(src, dst, normed_ref, acc, up_ref, down_ref):
    res_f = src[...].astype(F32)
    normed_ref[...] = norm_parts(res_f)[0].astype(BF16)
    acc[...] = res_f

    def body(t, carry):
        sl = lanes(t, FWD_TILE)
        pre = dot_nn(normed_ref[...], up_ref[:, sl])
        act = (pre * gelu_parts(pre)[1]).astype(BF16)
        acc[...] += dot_nn(act, down_ref[sl, :])
        return carry
    lax.fori_loop(0, HID_TWO // FWD_TILE, body, 0)
    dst[...] = acc[...].astype(BF16)


def image_rows():
    image = lax.broadcasted_iota(jnp.int32, (8, ROWS), 0)
    row = lax.broadcasted_iota(jnp.int32, (8, ROWS), 1)
    inside = (row >= image * MERGED) & (row < (image + 1) * MERGED)
    return jnp.where(inside, 1.0, 0.0).astype(BF16)


def pooled_norm(resid):
    pooled = dot_nn(image_rows(), resid) * (1.0 / MERGED)
    return norm_parts(pooled)


UNIT = 1024
N_UNITS = 9
SHARE_ROWS = N_UNITS * UNIT
CLASS_PAD = 1024
DEVS = 8
SUBLANES = 8
LAST = N_UNITS - 1
HELD = 4
PAIR_OUT, FIRST_OUT, SECOND_OUT, SECOND_BACK, FIRST_BACK, PAIR_BACK = range(6)


class Links:
    def __init__(self, own, final, land1, land2, sems):
        self.own, self.final, self.land1, self.land2, self.sems = own, final, land1, land2, sems
        me = lax.axis_index('data')
        self.me = me
        self.core, self.x, self.y = lax.rem(me, 2), lax.rem(me // 2, 2), me // 4
        self.pair = me + 1 - 2 * self.core
        self.x_peer = me + 2 - 4 * self.x
        self.y_peer = me + 4 - 8 * self.y

    def rows(self, unit, offset, size):
        return pl.ds(pl.multiple_of(unit * UNIT + offset, SHARD), size)

    def half(self, unit, offset, size):
        return self.rows(unit, self.core * WIDE + offset, size)

    def copy(self, unit, phase, lane, src, dst, peer):
        return pltpu.make_async_remote_copy(
            src_ref=src, dst_ref=dst, send_sem=self.sems.at[unit, phase, lane, 0], recv_sem=self.sems.at[unit, phase, lane, 1],
            device_id=(peer,), device_id_type=pl.DeviceIdType.MESH)

    def copies(self, unit, phase):
        x, y = self.x, self.y
        own, final = self.own, self.final
        if phase == PAIR_OUT:
            sl = self.rows(unit, (1 - self.core) * WIDE, WIDE)
            return [self.copy(unit, PAIR_OUT, 0, own.at[sl], final.at[sl], self.pair)]
        if phase == FIRST_OUT:
            land = lambda k: self.land1.at[pl.ds(pl.multiple_of(unit * TILE + k * WIDTH, WIDTH), WIDTH)]
            return [self.copy(unit, FIRST_OUT, 0, own.at[self.half(unit, (1 - x) * WIDTH, WIDTH)], land(0), self.x_peer),
                    self.copy(unit, FIRST_OUT, 1, own.at[self.half(unit, TILE + (1 - y) * WIDTH, WIDTH)], land(1), self.y_peer)]
        if phase == SECOND_OUT:
            land = lambda k: self.land2.at[pl.ds(pl.multiple_of(unit * WIDTH + k * SHARD, SHARD), SHARD)]
            return [self.copy(unit, SECOND_OUT, 0, own.at[self.half(unit, x * WIDTH + (1 - y) * SHARD, SHARD)], land(0), self.y_peer),
                    self.copy(unit, SECOND_OUT, 1, own.at[self.half(unit, TILE + y * WIDTH + (1 - x) * SHARD, SHARD)], land(1), self.x_peer)]
        if phase == SECOND_BACK:
            first = self.half(unit, x * WIDTH + y * SHARD, SHARD)
            second = self.half(unit, TILE + y * WIDTH + x * SHARD, SHARD)
            return [self.copy(unit, SECOND_BACK, 0, final.at[first], final.at[first], self.y_peer),
                    self.copy(unit, SECOND_BACK, 1, final.at[second], final.at[second], self.x_peer)]
        if phase == FIRST_BACK:
            first, second = self.half(unit, x * WIDTH, WIDTH), self.half(unit, TILE + y * WIDTH, WIDTH)
            return [self.copy(unit, FIRST_BACK, 0, final.at[first], final.at[first], self.x_peer),
                    self.copy(unit, FIRST_BACK, 1, final.at[second], final.at[second], self.y_peer)]
        sl = self.half(unit, 0, WIDE)
        return [self.copy(unit, PAIR_BACK, 0, final.at[sl], final.at[sl], self.pair)]

    def start(self, unit, phase):
        for copy in self.copies(unit, phase):
            copy.start()

    def wait(self, unit, phase):
        for copy in self.copies(unit, phase):
            copy.wait()

    def reduce_pair(self, unit):
        self.wait(unit, PAIR_OUT)
        x, y = self.x, self.y
        for offset in ((1 - x) * WIDTH, TILE + (1 - y) * WIDTH, x * WIDTH, TILE + y * WIDTH):
            sl = self.half(unit, offset, WIDTH)
            self.own[sl, :] = self.own[sl, :] + self.final[sl, :]
        self.start(unit, FIRST_OUT)

    def reduce_first(self, unit):
        self.wait(unit, FIRST_OUT)
        x, y = self.x, self.y
        for keep in (False, True):
            for lane, base, here, there in ((0, x * WIDTH, y, 0), (1, TILE + y * WIDTH, x, WIDTH)):
                part = here if keep else 1 - here
                sl = self.half(unit, base + part * SHARD, SHARD)
                land = pl.ds(pl.multiple_of(unit * TILE + there + part * SHARD, SHARD), SHARD)
                self.own[sl, :] = self.own[sl, :] + self.land1[land, :]
        self.start(unit, SECOND_OUT)

    def reduce_second(self, unit):
        self.wait(unit, SECOND_OUT)
        for lane, offset in ((0, self.x * WIDTH + self.y * SHARD), (1, TILE + self.y * WIDTH + self.x * SHARD)):
            sl = self.half(unit, offset, SHARD)
            land = pl.ds(pl.multiple_of(unit * WIDTH + lane * SHARD, SHARD), SHARD)
            self.final[sl, :] = self.own[sl, :] + self.land2[land, :]

    def forward(self, unit, phase):
        self.wait(unit, phase)
        self.start(unit, phase + 1)


def train_kernel(x_hbm, labels_ref, up1_hbm, dn1_hbm, mg_hbm, up2_hbm, dn2_hbm, hd_hbm,
                 sums_hbm, head_hbm,
                 x_v, x_f32, st_up1, st_dn1, st_mg, st_up2, st_dn2,
                 up1, dn1, mg, up2, dn2, hd,
                 r0, r1, r2, s0, s1, normed_ref, acc, grad_a, grad_b, sems,
                 du1, dv1, own, final, land1, land2, factors, g_hd, link_sems, factor_sems, out_sems):
    links = Links(own, final, land1, land2, link_sems)
    me = links.me
    st_hd = st_dn2.at[pl.ds(0, CLASSES)]
    copies = [pltpu.make_async_copy(src, dst, sems.at[i]) for i, (src, dst) in enumerate((
        (x_hbm, x_v), (up1_hbm, st_up1), (dn1_hbm, st_dn1), (mg_hbm, st_mg),
        (up2_hbm.at[0], st_up2), (dn2_hbm.at[0], st_dn2),
        (up2_hbm.at[1], st_up2), (dn2_hbm.at[1], st_dn2), (hd_hbm, st_hd)))]
    for i in range(6):
        copies[i].start()
    barrier = pltpu.get_barrier_semaphore()
    for k in range(1, DEVS):
        pl.semaphore_signal(barrier, inc=1, device_id=(lax.rem(me + k, DEVS),), device_id_type=pl.DeviceIdType.MESH)
    copies[0].wait()
    permute_tokens(x_v, x_f32, r0)
    copies[1].wait()
    copies[2].wait()
    for n in range(2):
        cast_rows(up1.at[n], st_up1.at[n], WIDTH, SHARD)
        cast_rows(dn1.at[n], st_dn1.at[n], WIDE, TILE)
    stage_one_forward(r0, r1, r2, up1, dn1)
    copies[3].wait()
    cast_rows(mg, st_mg, WIDE, SHARD)
    s0[...] = dot_nn(r2[...], mg[...]).astype(BF16)
    s2 = grad_a
    for n, (src, dst) in enumerate(((s0, s1), (s1, s2))):
        copies[4 + 2 * n].wait()
        cast_rows(up2.at[n], st_up2, WIDE, 16)
        if n == 0:
            copies[6].start()
        copies[5 + 2 * n].wait()
        cast_rows(dn2.at[n], st_dn2, 2048, SHARD)
        copies[7 + n].start()
        stage_two_block(src, dst, normed_ref, acc, up2.at[n], dn2.at[n])
    copies[8].wait()
    cast_rows(hd, st_hd, 992, 32)
    hd[992:CLASSES, :] = st_hd[992:CLASSES, :].astype(BF16)
    hd[CLASSES:, :] = jnp.zeros((CLASS_PAD - CLASSES, WIDE), BF16)
    head_normed, head_rstd = pooled_norm(s2[...])
    head_b = head_normed.astype(BF16)
    class_id = lax.broadcasted_iota(jnp.int32, (SUBLANES, CLASS_PAD), 1)
    row_id = lax.broadcasted_iota(jnp.int32, (SUBLANES, CLASS_PAD), 0)
    logits = jnp.where(class_id < CLASSES, dot_nt(head_b, hd[...]), -jnp.inf)
    top = jnp.max(logits, axis=-1, keepdims=True)
    expd = jnp.exp(logits - top)
    probs = expd / jnp.sum(expd, axis=-1, keepdims=True)
    label = jnp.zeros((SUBLANES, CLASS_PAD), jnp.int32)
    for i in range(IMGS):
        label = jnp.where(row_id == i, labels_ref[i], label)
    onehot = jnp.where(class_id == label, 1.0, 0.0)
    grad_logits = jnp.where(row_id < IMGS, (probs - onehot) * (1.0 / (IMGS * DEVS)), 0.0).astype(BF16)
    factors[me, :, :WIDE] = head_b
    factors[me, :, WIDE:] = grad_logits
    grad_pooled = norm_back(dot_nn(grad_logits, hd[...]), head_normed, head_rstd) * (1.0 / MERGED)
    grad_a[...] = dot_tn(image_rows(), grad_pooled.astype(BF16)).astype(BF16)

    pl.semaphore_wait(barrier, DEVS - 1)

    def factor_copy(k):
        return pltpu.make_async_remote_copy(
            src_ref=factors.at[me], dst_ref=factors.at[me], send_sem=factor_sems.at[k, 0], recv_sem=factor_sems.at[k, 1],
            device_id=(lax.rem(me + k, DEVS),), device_id_type=pl.DeviceIdType.MESH)

    grads = (grad_a, grad_b)
    for step, n in enumerate((1, 0)):
        g_in, g_out = grads[step], grads[1 - step]
        src = (s0, s1)[n]
        normed_ref[...] = norm_parts(src[...].astype(F32))[0].astype(BF16)
        acc[...] = jnp.zeros_like(acc)

        def tile(t, row, n=n, g_in=g_in):
            sl = lanes(t, TILE)
            pre = dot_nn(normed_ref[...], up2[n, :, sl])
            square, half = gelu_parts(pre)
            act = (pre * half).astype(BF16)
            grad_pre = (gelu_slope(pre, square, half) * dot_nt(g_in[...], dn2[n, sl, :])).astype(BF16)
            own[pl.ds(row + TILE, TILE), :] = dot_tn(act, g_in[...]).astype(BF16)
            grad_up = dot_tn(normed_ref[...], grad_pre).astype(BF16)
            own[pl.ds(row, TILE), :TILE] = grad_up[:TILE]
            own[pl.ds(row, TILE), TILE:] = grad_up[TILE:]
            acc[...] += dot_nt(grad_pre, up2[n, :, sl])

        def body(p, carry, step=step, tile=tile):
            unit = step * 4 + p
            row = pl.multiple_of(unit * UNIT, UNIT)

            tile(2 * p, row)
            if step:
                links.reduce_pair(unit - 1)
            else:
                pl.when(p > 0)(lambda: links.reduce_pair(unit - 1))
            tile(2 * p + 1, row + WIDE)
            if step:
                links.reduce_first(unit - 4)
            links.start(unit, PAIR_OUT)
            return carry
        if step == 0:
            for k in range(1, DEVS):
                factor_copy(k).start()
        lax.fori_loop(0, N_TILES // 2, body, 0)
        normed_f, rstd = norm_parts(src[...].astype(F32))
        g_out[...] = (norm_back(acc[...], normed_f, rstd) + g_in[...].astype(F32)).astype(BF16)
    own[LAST * UNIT:LAST * UNIT + WIDE, :] = dot_tn(r2[...], grad_a[...]).astype(BF16)
    grad_b[...] = dot_nt(grad_a[...], mg[...]).astype(BF16)

    def out_copy(unit):
        rows = pl.ds(unit * UNIT, UNIT)
        return pltpu.make_async_copy(final.at[rows], sums_hbm.at[rows], out_sems.at[unit])

    def reduced(unit):
        links.reduce_second(unit)
        links.start(unit, SECOND_BACK)

    def finish(unit):
        links.wait(unit, PAIR_BACK)
        out_copy(unit).start()

    def back_first(unit):
        links.forward(unit, SECOND_BACK)

    def back_pair(unit):
        links.forward(unit, FIRST_BACK)

    def run_all(steps):
        for action, unit in steps:
            action(unit)

    links.reduce_pair(7)
    first = links.reduce_first
    slots = {1: (((reduced, 0), (reduced, 1), (reduced, 2), (first, 4)), ((first, 5),), ((reduced, 3),), ((first, 6), (back_first, 0))),
             0: (((back_first, 1),), ((back_first, 2),), ((reduced, 4),), ((first, 7),))}

    for n, src, g_in, g_out in ((1, r1, grad_b, grad_a), (0, r0, grad_a, grad_b)):
        du1[...] = jnp.zeros_like(du1)
        dv1[...] = jnp.zeros_like(dv1)

        def body(j, carry, n=n, src=src, g_in=g_in, g_out=g_out):
            sl = lanes(j, WIDTH)
            normed_f, rstd = norm_parts(src[:, sl].astype(F32))
            normed = normed_f.astype(BF16)
            grad = g_in[:, sl]
            pre = dot_nn(normed, up1[n])
            square, half = gelu_parts(pre)
            act = (pre * half).astype(BF16)
            grad_pre = (gelu_slope(pre, square, half) * dot_nt(grad, dn1[n])).astype(BF16)
            dv1[...] += dot_tn(grad, act)
            du1[...] += dot_tn(normed, grad_pre)
            if n:
                back = norm_back(dot_nt(grad_pre, up1[n]), normed_f, rstd)
                g_out[:, sl] = (back + grad.astype(F32)).astype(BF16)
            for k, steps in enumerate(slots[n]):
                pl.when(j == k)(lambda steps=steps: run_all(steps))
            return carry
        lax.fori_loop(0, 4, body, 0)
        base = LAST * UNIT + WIDE + n * WIDTH
        own[base:base + WIDTH, :] = du1[...].astype(BF16)
        own[base + TILE:base + TILE + WIDTH, :] = dv1[...].astype(BF16)
    links.start(LAST, PAIR_OUT)

    for k in range(1, DEVS):
        factor_copy(k).wait()

    def head_tile(c, carry):
        sl = pl.ds(pl.multiple_of(WIDE + c * WIDTH, WIDTH), WIDTH)
        total = jnp.zeros((WIDTH, WIDE), F32)
        for d in range(DEVS):
            total += dot_tn(factors[d, :, sl], factors[d, :, :WIDE]).astype(BF16).astype(F32)
        g_hd[pl.ds(pl.multiple_of(c * WIDTH, WIDTH), WIDTH), :] = total.astype(BF16)
        return carry
    half_tiles = CLASS_PAD // WIDTH // 2
    lax.fori_loop(0, half_tiles, head_tile, 0)
    run_all(((links.reduce_pair, LAST), (reduced, 5), (back_first, 3)))
    lax.fori_loop(half_tiles, 2 * half_tiles, head_tile, 0)
    head_copy = pltpu.make_async_copy(g_hd, head_hbm, factor_sems.at[0, 0])
    head_copy.start()
    run_all(((reduced, 6), (first, LAST), (back_pair, 0), (back_pair, 1), (finish, 0), (back_pair, 2), (finish, 1), (reduced, 7),
             (reduced, LAST), (back_first, 4), (finish, 2), (back_first, 5), (back_pair, 3), (back_first, 6), (back_first, LAST),
             (finish, 3), (back_pair, 4), (back_first, 7), (back_pair, 5), (finish, 4), (back_pair, LAST), (back_pair, 6), (finish, 5),
             (finish, LAST), (back_pair, 7), (finish, 6), (finish, 7)))
    for unit in range(N_UNITS):
        out_copy(unit).wait()
    head_copy.wait()


def sum_rows(tile):
    rows, cols = tile.shape
    return jnp.sum(tile.reshape(rows // 8, 8, cols), axis=0)


def lars_matrix(steps, piece, cols, tails=()):
    zero = jnp.zeros((8, cols), F32)

    def norms(i, carry):
        w, _, g, _ = piece(i)
        w, g = w[...], g[...].astype(F32)
        return carry[0] + sum_rows(w * w), carry[1] + sum_rows(g * g)
    w_acc, g_acc = lax.fori_loop(0, steps, norms, (zero, zero))
    for w, _, g, _ in tails:
        w, g = w[...], g[...].astype(F32)
        w_acc, g_acc = w_acc + sum_rows(w * w), g_acc + sum_rows(g * g)
    w_norm = jnp.sqrt(jnp.sum(jnp.sum(w_acc, axis=0, keepdims=True), axis=1, keepdims=True))
    g_norm = jnp.sqrt(jnp.sum(jnp.sum(g_acc, axis=0, keepdims=True), axis=1, keepdims=True))
    scale = TRUST * (w_norm / g_norm)

    def update_piece(w, v, g, b):
        new_v = MOMENTUM * v[...] + scale * g[...].astype(F32)
        new_w = w[...] - new_v
        v[...] = new_v
        w[...] = new_w
        b[...] = new_w.astype(BF16)

    def update(i, carry):
        update_piece(*piece(i))
        return carry
    lax.fori_loop(0, steps, update, 0)
    for tail in tails:
        update_piece(*tail)


def row_pieces(w, v, g, b, step):
    def piece(i):
        sl = pl.ds(pl.multiple_of(i * step, step), step)
        return w.at[sl], v.at[sl], g.at[sl], b.at[sl]
    return piece


def up_pieces(w, v, g, b):
    def piece(i):
        h, part = i // 2, lax.rem(i, 2)
        rows, cols = lanes(part, 256), lanes(h, 256)
        g_rows = pl.ds(pl.multiple_of(h * 512, 512), 256)
        return w.at[rows, cols], v.at[rows, cols], g.at[g_rows, rows], b.at[rows, cols]
    return piece


def down_pieces(w, v, g, b):
    def piece(i):
        h, part = i // 2, lax.rem(i, 2)
        rows = pl.ds(pl.multiple_of(i * 128, 128), 128)
        g_rows = pl.ds(pl.multiple_of(h * 512 + 256 + part * 128, 128), 128)
        return w.at[rows], v.at[rows], g.at[g_rows], b.at[rows]
    return piece


def start_all(copies):
    for copy in copies:
        copy.start()


def wait_all(copies):
    for copy in copies:
        copy.wait()


class Pair:
    def __init__(self, w, v, out_w, out_v, buf_w, buf_v, sems, slot):
        self.buf_w, self.buf_v = buf_w, buf_v
        ends = ((w, buf_w), (v, buf_v)), ((buf_w, out_w), (buf_v, out_v))
        self.loads, self.stores = ([pltpu.make_async_copy(src, dst, sems.at[slot, k, i]) for i, (src, dst) in enumerate(part)]
                                   for k, part in enumerate(ends))

    def update(self, steps, make, grad, cast, cols, *rest, tails=()):
        wait_all(self.loads)
        lars_matrix(steps, make(self.buf_w, self.buf_v, grad, cast, *rest), cols, tails)
        start_all(self.stores)


def next_kernel(x_hbm, up1_hbm, dn1_hbm, mg_hbm, up2_hbm, dn2_hbm, hd_hbm,
                vup1_hbm, vdn1_hbm, vmg_hbm, vup2_hbm, vdn2_hbm, vhd_hbm, sums_hbm, ghd_hbm,
                logits_ref, o_up1, o_dn1, o_mg, o_up2, o_dn2, o_hd, ov_up1, ov_dn1, ov_mg, ov_up2, ov_dn2, ov_hd,
                x_v, x_f32, wb_up1, wb_dn1, wb_mg, wb_up2, wb_dn2, vb_up1, vb_dn1, vb_mg, vb_up2, vb_dn2,
                gb_small, gb_turn, gb_two, gb_hd, up1, dn1, mg, up2, dn2, hd, r0, s0, s1, normed_ref, acc, sems, sem_g):
    def pair(n, slot, *refs):
        return Pair(*(ref.at[n] for ref in refs), sems, slot)

    ups = [pair(n, n, up1_hbm, vup1_hbm, o_up1, ov_up1, wb_up1, vb_up1) for n in range(2)]
    downs = [pair(n, 2 + n, dn1_hbm, vdn1_hbm, o_dn1, ov_dn1, wb_dn1, vb_dn1) for n in range(2)]
    merge = Pair(mg_hbm, vmg_hbm, o_mg, ov_mg, wb_mg, vb_mg, sems, 4)
    wide_ups = [pair(n, 5 + n, up2_hbm, vup2_hbm, o_up2, ov_up2, wb_up2, vb_up2) for n in range(2)]
    wide_downs = [pair(n, 7 + n, dn2_hbm, vdn2_hbm, o_dn2, ov_dn2, wb_dn2, vb_dn2) for n in range(2)]
    wb_hd, vb_hd = (buf.at[1, pl.ds(0, CLASSES)] for buf in (wb_dn2, vb_dn2))
    head = Pair(hd_hbm, vhd_hbm, o_hd, ov_hd, wb_hd, vb_hd, sems, 9)
    g_copies = [pltpu.make_async_copy(src, dst, sem_g.at[i]) for i, (src, dst) in enumerate((
        (x_hbm, x_v), (sums_hbm.at[pl.ds(LAST * UNIT, UNIT)], gb_small), (ghd_hbm, gb_hd),
        (sums_hbm.at[pl.ds(HELD * UNIT, HELD * UNIT)], gb_two), (sums_hbm.at[pl.ds(0, HELD * UNIT)], gb_two)))]
    x_copy, g_small, g_head, g_first, g_second = g_copies
    start_all((x_copy, g_small))
    for each in ups + downs + [merge]:
        start_all(each.loads)
    g_head.start()
    start_all(head.loads)
    g_first.start()
    for each in (wide_ups[0], wide_downs[0], wide_ups[1]):
        start_all(each.loads)
    x_copy.wait()
    permute_tokens(x_v, x_f32, r0)
    g_small.wait()
    for n in range(2):
        ups[n].update(2, row_pieces, gb_small.at[pl.ds(WIDE + n * WIDTH, WIDTH)], up1.at[n], WIDE, SHARD)
        gb_turn[...] = gb_small[pl.ds(WIDE + TILE + n * WIDTH, WIDTH), :].astype(F32).T
        downs[n].update(4, row_pieces, gb_turn, dn1.at[n], WIDTH, WIDTH)
    merge.update(8, row_pieces, gb_small.at[pl.ds(0, WIDE)], mg, WIDE, SHARD)
    g_head.wait()
    tail = pl.ds(992, SUBLANES)
    head.update(31, row_pieces, gb_hd, hd, WIDE, 32, tails=[(wb_hd.at[tail], vb_hd.at[tail], gb_hd.at[tail], hd.at[tail])])
    stage_one_forward(r0, s0, s1, up1, dn1)
    wait_all(head.stores)
    start_all(wide_downs[1].loads)
    s0[...] = dot_nn(s1[...], mg[...]).astype(BF16)
    for n, (src, dst) in enumerate(((s0, s1), (s1, s0))):
        g_copies[3 + n].wait()
        wide_ups[n].update(16, up_pieces, gb_two, up2, TILE)
        wide_downs[n].update(16, down_pieces, gb_two, dn2, WIDE)
        if n == 0:
            g_second.start()
        stage_two_block(src, dst, normed_ref, acc, up2, dn2)
    head_b = pooled_norm(s0[...])[0].astype(BF16)
    logits_ref[...] = dot_nt(head_b, hd[...])[:IMGS]
    for each in ups + downs + [merge] + wide_ups + wide_downs:
        wait_all(each.stores)


W_SHAPES = ((2, 128, 512), (2, 512, 128), (512, 512), (2, 512, 2048), (2, 2048, 512), (CLASSES, 512))
BUF_SHAPES = W_SHAPES[:3] + ((512, 2048), (2048, 512), (CLASSES, 512))


def vmem(shape, dtype):
    return pltpu.VMEM(shape, dtype)


ANY_SPEC = pl.BlockSpec(memory_space=pl.ANY)
VMEM_SPEC = pl.BlockSpec(memory_space=pltpu.VMEM)


def act(dtype=BF16):
    return vmem((ROWS, WIDE), dtype)


def f32_outs(shapes):
    return [jax.ShapeDtypeStruct(shape, F32) for shape in shapes]


DMA = pltpu.SemaphoreType.DMA


def run_train(x_now, labels, params):
    return pl.pallas_call(
        train_kernel,
        out_shape=[jax.ShapeDtypeStruct((rows, WIDE), BF16) for rows in (SHARE_ROWS, CLASS_PAD)],
        in_specs=[ANY_SPEC, pl.BlockSpec(memory_space=pltpu.SMEM)] + [ANY_SPEC] * 6,
        out_specs=[ANY_SPEC] * 2,
        scratch_shapes=[vmem((ROWS * 4, WIDTH), BF16), vmem((ROWS * 4, WIDTH), F32)]
        + [vmem(shape, F32) for shape in BUF_SHAPES[:5]] + [vmem(shape, BF16) for shape in W_SHAPES[:5]] + [vmem((CLASS_PAD, WIDE), BF16)]
        + [act()] * 6 + [act(F32), act(), act(), DMA((9,)), vmem((WIDTH, WIDE), F32), vmem((WIDTH, WIDE), F32)]
        + [vmem((rows, WIDE), BF16) for rows in (SHARE_ROWS, SHARE_ROWS, N_UNITS * TILE, N_UNITS * WIDTH)]
        + [vmem((DEVS, SUBLANES, WIDE + CLASS_PAD), BF16), vmem((CLASS_PAD, WIDE), BF16)]
        + [DMA((N_UNITS, 6, 2, 2)), DMA((DEVS, 2)), DMA((N_UNITS,))],
        compiler_params=pltpu.CompilerParams(vmem_limit_bytes=VMEM_BYTES, collective_id=0, has_side_effects=True),
        cost_estimate=pl.CostEstimate(flops=30_000_000_000, bytes_accessed=40_000_000, transcendentals=0),
        name='train_part',
    )(x_now, labels, *params)


def run_next(x_next, params, velocities, sums, head_sum):
    return pl.pallas_call(
        next_kernel,
        out_shape=f32_outs([(IMGS, CLASSES)] + list(W_SHAPES) * 2),
        in_specs=[ANY_SPEC] * 15,
        out_specs=[VMEM_SPEC] + [ANY_SPEC] * 12,
        scratch_shapes=[vmem((ROWS * 4, WIDTH), BF16), vmem((ROWS * 4, WIDTH), F32)]
        + [vmem(shape, F32) for shape in W_SHAPES[:5]] * 2
        + [vmem((UNIT, WIDE), BF16), vmem((WIDE, WIDTH), F32), vmem((HELD * UNIT, WIDE), BF16), vmem((CLASS_PAD, WIDE), BF16)]
        + [vmem(shape, BF16) for shape in BUF_SHAPES]
        + [act()] * 4 + [act(F32), DMA((10, 2, 2)), DMA((5,))],
        compiler_params=pltpu.CompilerParams(vmem_limit_bytes=VMEM_BYTES),
        cost_estimate=pl.CostEstimate(flops=10_000_000_000, bytes_accessed=100_000_000, transcendentals=0),
        name='next_part',
    )(x_next, *params, *velocities, sums, head_sum)


def turn_head(arrays):
    return (*arrays[:5], arrays[5].T)


def solution(mesh):
    def local_step(x_now, labels_now, x_next, *weights):
        params, velocities = turn_head(weights[:6]), turn_head(weights[6:])
        sums, head_sum = run_train(x_now.reshape(ROWS * 4, WIDTH), labels_now, params)
        outs = run_next(x_next.reshape(ROWS * 4, WIDTH), params, velocities, sums, head_sum)
        return (outs[0], *turn_head(outs[1:7]), *turn_head(outs[7:]))

    split = P('data')
    in_specs = (split, split, split) + (P(),) * 12
    out_specs = (split,) + (P(),) * 12
    return jax.shard_map(local_step, mesh=mesh, in_specs=in_specs, out_specs=out_specs, check_vma=False)
```

profile of v0, /device:TPU:0, one launch (start us, length us, event | category | flops | bytes accessed | tf_op | source)
XLA Modules:
  0.0 162.0 jit_solution(1597284763690558841)
XLA Ops:
  0.6 121.5 %train_part.1 = (bf16[9216,512]{1,0:T(8,128)(2,1)}, bf16[1024,512]{1,0:T(8,128)(2,1)}) custom-call(bf16[3136,128]{1,0:T(8,128)(2,1)} %bitcast.12, s32[4]{0:T(128)} %labels_ref.1, f32[2,128,512]{2,1,0:T(8,128)} %up1_hbm.3, f32[2,512,128]{2,1,0:T(8,128)} %dn1_hbm.3, f32[512,512]{1,0:T(8,128)} %mg_hbm.3, f32[2,512,2048]{2,1,0:T(8,128)} %up2_hbm.3, ...), custom_call_target="tpu_custom_call" | custom-call | flops 30000001024 | bytes 40000000 | tf_op jit(solution)/shard_map/train_part/pallas_call | solution.py:575
  122.1 39.7 %next_part.1 = (f32[4,1000]{1,0:T(4,128)}, f32[2,128,512]{2,1,0:T(8,128)}, f32[2,512,128]{2,1,0:T(8,128)}, f32[512,512]{1,0:T(8,128)}, f32[2,512,2048]{2,1,0:T(8...) custom-call(bf16[3136,128]{1,0:T(8,128)(2,1)} %bitcast.9, ...), custom_call_target="tpu_custom_call" | custom-call | flops 10000000000 | bytes 100000000 | tf_op jit(solution)/shard_map/next_part/pallas_call | solution.py:593
where the time goes:
time: 162 us
  Pallas kernels  161 us (99%)
    pallas_call x1, Pallas kernels, run_train(): pl.pallas_call(train_kernel, out_shape=[jax.ShapeDtypeStruct((rows, WIDE)...  121 us
    pallas_call x1, Pallas kernels, run_next(): pl.pallas_call(next_kernel, out_shape=f32_outs([(IMGS, CLASSES)] + list(W...  39.7 us

commit v1 on v0

--- a/solution.py
+++ b/solution.py
@@ -234,15 +234,14 @@
         (x_hbm, x_v), (up1_hbm, st_up1), (dn1_hbm, st_dn1), (mg_hbm, st_mg),
         (up2_hbm.at[0], st_up2), (dn2_hbm.at[0], st_dn2),
         (up2_hbm.at[1], st_up2), (dn2_hbm.at[1], st_dn2), (hd_hbm, st_hd)))]
-    for i in range(6):
-        copies[i].start()
+    start_all(copies[:3])
     barrier = pltpu.get_barrier_semaphore()
     for k in range(1, DEVS):
         pl.semaphore_signal(barrier, inc=1, device_id=(lax.rem(me + k, DEVS),), device_id_type=pl.DeviceIdType.MESH)
     copies[0].wait()
     permute_tokens(x_v, x_f32, r0)
-    copies[1].wait()
-    copies[2].wait()
+    wait_all(copies[1:3])
+    start_all(copies[3:6])
     for n in range(2):
         cast_rows(up1.at[n], st_up1.at[n], WIDTH, SHARD)
         cast_rows(dn1.at[n], st_dn1.at[n], WIDE, TILE)
@@ -513,31 +512,34 @@
         (sums_hbm.at[pl.ds(HELD * UNIT, HELD * UNIT)], gb_two), (sums_hbm.at[pl.ds(0, HELD * UNIT)], gb_two)))]
     x_copy, g_small, g_head, g_first, g_second = g_copies
     start_all((x_copy, g_small))
-    for each in ups + downs + [merge]:
+    for each in ups + downs:
         start_all(each.loads)
+    x_copy.wait()
+    start_all(merge.loads)
+    permute_tokens(x_v, x_f32, r0)
+    g_small.wait()
     g_head.start()
     start_all(head.loads)
-    g_first.start()
-    for each in (wide_ups[0], wide_downs[0], wide_ups[1]):
-        start_all(each.loads)
-    x_copy.wait()
-    permute_tokens(x_v, x_f32, r0)
-    g_small.wait()
     for n in range(2):
         ups[n].update(2, row_pieces, gb_small.at[pl.ds(WIDE + n * WIDTH, WIDTH)], up1.at[n], WIDE, SHARD)
         gb_turn[...] = gb_small[pl.ds(WIDE + TILE + n * WIDTH, WIDTH), :].astype(F32).T
         downs[n].update(4, row_pieces, gb_turn, dn1.at[n], WIDTH, WIDTH)
     merge.update(8, row_pieces, gb_small.at[pl.ds(0, WIDE)], mg, WIDE, SHARD)
+    g_first.start()
+    start_all(wide_ups[0].loads)
     g_head.wait()
     tail = pl.ds(992, SUBLANES)
     head.update(31, row_pieces, gb_hd, hd, WIDE, 32, tails=[(wb_hd.at[tail], vb_hd.at[tail], gb_hd.at[tail], hd.at[tail])])
+    start_all(wide_downs[0].loads)
     stage_one_forward(r0, s0, s1, up1, dn1)
     wait_all(head.stores)
-    start_all(wide_downs[1].loads)
+    start_all(wide_ups[1].loads)
     s0[...] = dot_nn(s1[...], mg[...]).astype(BF16)
     for n, (src, dst) in enumerate(((s0, s1), (s1, s0))):
         g_copies[3 + n].wait()
         wide_ups[n].update(16, up_pieces, gb_two, up2, TILE)
+        if n == 0:
+            start_all(wide_downs[1].loads)
         wide_downs[n].update(16, down_pieces, gb_two, dn2, WIDE)
         if n == 0:
             g_second.start()

time: 162 us -> 162 us (level)
  no operation moved by 1% of the time
where the time goes in v1:
time: 162 us
  Pallas kernels  161 us (99%)
    pallas_call x1, Pallas kernels, run_train(): pl.pallas_call(train_kernel, out_shape=[jax.ShapeDtypeStruct((rows, WIDE)...  121 us
    pallas_call x1, Pallas kernels, run_next(): pl.pallas_call(next_kernel, out_shape=f32_outs([(IMGS, CLASSES)] + list(W...  39.7 us

profile of v1, /device:TPU:0, one launch (start us, length us, event | category | flops | bytes accessed | tf_op | source)
XLA Modules:
  0.0 162.0 jit_solution(9329016512666083753)
XLA Ops:
  0.6 121.4 %train_part.1 = (bf16[9216,512]{1,0:T(8,128)(2,1)}, bf16[1024,512]{1,0:T(8,128)(2,1)}) custom-call(bf16[3136,128]{1,0:T(8,128)(2,1)} %bitcast.12, s32[4]{0:T(128)} %labels_ref.1, f32[2,128,512]{2,1,0:T(8,128)} %up1_hbm.3, f32[2,512,128]{2,1,0:T(8,128)} %dn1_hbm.3, f32[512,512]{1,0:T(8,128)} %mg_hbm.3, f32[2,512,2048]{2,1,0:T(8,128)} %up2_hbm.3, ...), custom_call_target="tpu_custom_call" | custom-call | flops 30000001024 | bytes 40000000 | tf_op jit(solution)/shard_map/train_part/pallas_call | solution.py:577
  122.1 39.7 %next_part.1 = (f32[4,1000]{1,0:T(4,128)}, f32[2,128,512]{2,1,0:T(8,128)}, f32[2,512,128]{2,1,0:T(8,128)}, f32[512,512]{1,0:T(8,128)}, f32[2,512,2048]{2,1,0:T(8...) custom-call(bf16[3136,128]{1,0:T(8,128)(2,1)} %bitcast.9, ...), custom_call_target="tpu_custom_call" | custom-call | flops 10000000000 | bytes 100000000 | tf_op jit(solution)/shard_map/next_part/pallas_call | solution.py:595

commit v2 on v1

--- a/solution.py
+++ b/solution.py
@@ -132,7 +132,34 @@
 SUBLANES = 8
 LAST = N_UNITS - 1
 HELD = 4
+MATRICES = 10
 PAIR_OUT, FIRST_OUT, SECOND_OUT, SECOND_BACK, FIRST_BACK, PAIR_BACK = range(6)
+
+
+def start_all(copies):
+    for copy in copies:
+        copy.start()
+
+
+def wait_all(copies):
+    for copy in copies:
+        copy.wait()
+
+
+def sum_rows(tile):
+    rows, cols = tile.shape
+    return jnp.sum(tile.reshape(rows // 8, 8, cols), axis=0)
+
+
+def square_sum(ref, start, rows, step):
+    def body(i, total):
+        part = ref[pl.ds(pl.multiple_of(start + i * step, step), step), :].astype(F32)
+        return total + sum_rows(part * part)
+    return lax.fori_loop(0, rows // step, body, jnp.zeros((SUBLANES, ref.shape[1]), F32))
+
+
+def total_of(tile):
+    return jnp.sum(jnp.sum(tile, axis=0, keepdims=True), axis=1, keepdims=True)
 
 
 class Links:
@@ -222,11 +249,11 @@
 
 
 def train_kernel(x_hbm, labels_ref, up1_hbm, dn1_hbm, mg_hbm, up2_hbm, dn2_hbm, hd_hbm,
-                 sums_hbm, head_hbm,
+                 sums_hbm, head_hbm, scale_ref,
                  x_v, x_f32, st_up1, st_dn1, st_mg, st_up2, st_dn2,
                  up1, dn1, mg, up2, dn2, hd,
                  r0, r1, r2, s0, s1, normed_ref, acc, grad_a, grad_b, sems,
-                 du1, dv1, own, final, land1, land2, factors, g_hd, link_sems, factor_sems, out_sems):
+                 du1, dv1, own, final, land1, land2, factors, g_hd, w_sums, g_sums, link_sems, factor_sems, out_sems):
     links = Links(own, final, land1, land2, link_sems)
     me = links.me
     st_hd = st_dn2.at[pl.ds(0, CLASSES)]
@@ -341,6 +368,42 @@
     def finish(unit):
         links.wait(unit, PAIR_BACK)
         out_copy(unit).start()
+        start = unit * UNIT
+        if unit < LAST:
+            for k in range(4):
+                matrix = (6 if unit < HELD else 5) + 2 * (k % 2)
+                g_sums[matrix] += square_sum(final, start + k * TILE, TILE, SHARD)
+        else:
+            g_sums[4] = square_sum(final, start, WIDE, SHARD)
+            for k in range(4):
+                g_sums[k] = square_sum(final, start + WIDE + k * WIDTH, WIDTH, SHARD)
+
+    def weigh(matrix, ref, rows, step):
+        w_sums[pl.ds(matrix * SUBLANES, SUBLANES), :] = jnp.broadcast_to(total_of(square_sum(ref, 0, rows, step)), (SUBLANES, WIDTH))
+
+    reloads = [pltpu.make_async_copy(src, dst, sems.at[9 + i]) for i, (src, dst) in enumerate((
+        (up2_hbm.at[0], st_up2), (dn2_hbm.at[0], st_dn2), (dn2_hbm.at[1], st_dn2)))]
+
+    def weigh_small(_):
+        for n in range(2):
+            weigh(n, st_up1.at[n], WIDTH, SHARD)
+            weigh(2 + n, st_dn1.at[n], WIDE, WIDTH)
+        weigh(4, st_mg, WIDE, SHARD)
+        weigh(6, st_up2, WIDE, 16)
+        w_hd = square_sum(st_dn2, 0, 992, 32) + square_sum(st_dn2, 992, SUBLANES, SUBLANES)
+        w_sums[pl.ds(9 * SUBLANES, SUBLANES), :] = jnp.broadcast_to(total_of(w_hd), (SUBLANES, WIDTH))
+        start_all(reloads[:2])
+
+    def weigh_first(_):
+        wait_all(reloads[:2])
+        weigh(5, st_up2, WIDE, 16)
+        weigh(7, st_dn2, HID_TWO, SHARD)
+        reloads[2].start()
+
+    def weigh_second(_):
+        reloads[2].wait()
+        weigh(8, st_dn2, HID_TWO, SHARD)
+        g_sums[9] = square_sum(g_hd, 0, CLASS_PAD, SHARD)
 
     def back_first(unit):
         links.forward(unit, SECOND_BACK)
@@ -352,6 +415,7 @@
         for action, unit in steps:
             action(unit)
 
+    g_sums[...] = jnp.zeros_like(g_sums)
     links.reduce_pair(7)
     first = links.reduce_first
     slots = {1: (((reduced, 0), (reduced, 1), (reduced, 2), (first, 4)), ((first, 5),), ((reduced, 3),), ((first, 6), (back_first, 0))),
@@ -400,35 +464,19 @@
     lax.fori_loop(half_tiles, 2 * half_tiles, head_tile, 0)
     head_copy = pltpu.make_async_copy(g_hd, head_hbm, factor_sems.at[0, 0])
     head_copy.start()
-    run_all(((reduced, 6), (first, LAST), (back_pair, 0), (back_pair, 1), (finish, 0), (back_pair, 2), (finish, 1), (reduced, 7),
+    run_all(((reduced, 6), (weigh_small, 0), (first, LAST), (weigh_first, 0), (back_pair, 0), (back_pair, 1), (finish, 0), (weigh_second, 0), (back_pair, 2), (finish, 1), (reduced, 7),
              (reduced, LAST), (back_first, 4), (finish, 2), (back_first, 5), (back_pair, 3), (back_first, 6), (back_first, LAST),
              (finish, 3), (back_pair, 4), (back_first, 7), (back_pair, 5), (finish, 4), (back_pair, LAST), (back_pair, 6), (finish, 5),
              (finish, LAST), (back_pair, 7), (finish, 6), (finish, 7)))
+    for matrix in range(MATRICES):
+        sl = pl.ds(matrix * SUBLANES, SUBLANES)
+        scale_ref[sl, :] = TRUST * (jnp.sqrt(w_sums[sl, :]) / jnp.sqrt(total_of(g_sums[matrix])))
     for unit in range(N_UNITS):
         out_copy(unit).wait()
     head_copy.wait()
 
 
-def sum_rows(tile):
-    rows, cols = tile.shape
-    return jnp.sum(tile.reshape(rows // 8, 8, cols), axis=0)
-
-
-def lars_matrix(steps, piece, cols, tails=()):
-    zero = jnp.zeros((8, cols), F32)
-
-    def norms(i, carry):
-        w, _, g, _ = piece(i)
-        w, g = w[...], g[...].astype(F32)
-        return carry[0] + sum_rows(w * w), carry[1] + sum_rows(g * g)
-    w_acc, g_acc = lax.fori_loop(0, steps, norms, (zero, zero))
-    for w, _, g, _ in tails:
-        w, g = w[...], g[...].astype(F32)
-        w_acc, g_acc = w_acc + sum_rows(w * w), g_acc + sum_rows(g * g)
-    w_norm = jnp.sqrt(jnp.sum(jnp.sum(w_acc, axis=0, keepdims=True), axis=1, keepdims=True))
-    g_norm = jnp.sqrt(jnp.sum(jnp.sum(g_acc, axis=0, keepdims=True), axis=1, keepdims=True))
-    scale = TRUST * (w_norm / g_norm)
-
+def lars_matrix(steps, piece, scale, tails=()):
     def update_piece(w, v, g, b):
         new_v = MOMENTUM * v[...] + scale * g[...].astype(F32)
         new_w = w[...] - new_v
@@ -469,44 +517,35 @@
     return piece
 
 
-def start_all(copies):
-    for copy in copies:
-        copy.start()
-
-
-def wait_all(copies):
-    for copy in copies:
-        copy.wait()
-
-
 class Pair:
-    def __init__(self, w, v, out_w, out_v, buf_w, buf_v, sems, slot):
+    def __init__(self, w, v, out_w, out_v, buf_w, buf_v, sems, scales, slot):
         self.buf_w, self.buf_v = buf_w, buf_v
+        self.scale = scales.at[pl.ds(slot * SUBLANES, 1), pl.ds(0, 1)]
         ends = ((w, buf_w), (v, buf_v)), ((buf_w, out_w), (buf_v, out_v))
         self.loads, self.stores = ([pltpu.make_async_copy(src, dst, sems.at[slot, k, i]) for i, (src, dst) in enumerate(part)]
                                    for k, part in enumerate(ends))
 
-    def update(self, steps, make, grad, cast, cols, *rest, tails=()):
+    def update(self, steps, make, grad, cast, *rest, tails=()):
         wait_all(self.loads)
-        lars_matrix(steps, make(self.buf_w, self.buf_v, grad, cast, *rest), cols, tails)
+        lars_matrix(steps, make(self.buf_w, self.buf_v, grad, cast, *rest), self.scale[...], tails)
         start_all(self.stores)
 
 
 def next_kernel(x_hbm, up1_hbm, dn1_hbm, mg_hbm, up2_hbm, dn2_hbm, hd_hbm,
-                vup1_hbm, vdn1_hbm, vmg_hbm, vup2_hbm, vdn2_hbm, vhd_hbm, sums_hbm, ghd_hbm,
+                vup1_hbm, vdn1_hbm, vmg_hbm, vup2_hbm, vdn2_hbm, vhd_hbm, sums_hbm, ghd_hbm, scales,
                 logits_ref, o_up1, o_dn1, o_mg, o_up2, o_dn2, o_hd, ov_up1, ov_dn1, ov_mg, ov_up2, ov_dn2, ov_hd,
                 x_v, x_f32, wb_up1, wb_dn1, wb_mg, wb_up2, wb_dn2, vb_up1, vb_dn1, vb_mg, vb_up2, vb_dn2,
                 gb_small, gb_turn, gb_two, gb_hd, up1, dn1, mg, up2, dn2, hd, r0, s0, s1, normed_ref, acc, sems, sem_g):
     def pair(n, slot, *refs):
-        return Pair(*(ref.at[n] for ref in refs), sems, slot)
+        return Pair(*(ref.at[n] for ref in refs), sems, scales, slot)
 
     ups = [pair(n, n, up1_hbm, vup1_hbm, o_up1, ov_up1, wb_up1, vb_up1) for n in range(2)]
     downs = [pair(n, 2 + n, dn1_hbm, vdn1_hbm, o_dn1, ov_dn1, wb_dn1, vb_dn1) for n in range(2)]
-    merge = Pair(mg_hbm, vmg_hbm, o_mg, ov_mg, wb_mg, vb_mg, sems, 4)
+    merge = Pair(mg_hbm, vmg_hbm, o_mg, ov_mg, wb_mg, vb_mg, sems, scales, 4)
     wide_ups = [pair(n, 5 + n, up2_hbm, vup2_hbm, o_up2, ov_up2, wb_up2, vb_up2) for n in range(2)]
     wide_downs = [pair(n, 7 + n, dn2_hbm, vdn2_hbm, o_dn2, ov_dn2, wb_dn2, vb_dn2) for n in range(2)]
     wb_hd, vb_hd = (buf.at[1, pl.ds(0, CLASSES)] for buf in (wb_dn2, vb_dn2))
-    head = Pair(hd_hbm, vhd_hbm, o_hd, ov_hd, wb_hd, vb_hd, sems, 9)
+    head = Pair(hd_hbm, vhd_hbm, o_hd, ov_hd, wb_hd, vb_hd, sems, scales, 9)
     g_copies = [pltpu.make_async_copy(src, dst, sem_g.at[i]) for i, (src, dst) in enumerate((
         (x_hbm, x_v), (sums_hbm.at[pl.ds(LAST * UNIT, UNIT)], gb_small), (ghd_hbm, gb_hd),
         (sums_hbm.at[pl.ds(HELD * UNIT, HELD * UNIT)], gb_two), (sums_hbm.at[pl.ds(0, HELD * UNIT)], gb_two)))]
@@ -521,15 +560,15 @@
     g_head.start()
     start_all(head.loads)
     for n in range(2):
-        ups[n].update(2, row_pieces, gb_small.at[pl.ds(WIDE + n * WIDTH, WIDTH)], up1.at[n], WIDE, SHARD)
+        ups[n].update(2, row_pieces, gb_small.at[pl.ds(WIDE + n * WIDTH, WIDTH)], up1.at[n], SHARD)
         gb_turn[...] = gb_small[pl.ds(WIDE + TILE + n * WIDTH, WIDTH), :].astype(F32).T
-        downs[n].update(4, row_pieces, gb_turn, dn1.at[n], WIDTH, WIDTH)
-    merge.update(8, row_pieces, gb_small.at[pl.ds(0, WIDE)], mg, WIDE, SHARD)
+        downs[n].update(4, row_pieces, gb_turn, dn1.at[n], WIDTH)
+    merge.update(8, row_pieces, gb_small.at[pl.ds(0, WIDE)], mg, SHARD)
     g_first.start()
     start_all(wide_ups[0].loads)
     g_head.wait()
     tail = pl.ds(992, SUBLANES)
-    head.update(31, row_pieces, gb_hd, hd, WIDE, 32, tails=[(wb_hd.at[tail], vb_hd.at[tail], gb_hd.at[tail], hd.at[tail])])
+    head.update(31, row_pieces, gb_hd, hd, 32, tails=[(wb_hd.at[tail], vb_hd.at[tail], gb_hd.at[tail], hd.at[tail])])
     start_all(wide_downs[0].loads)
     stage_one_forward(r0, s0, s1, up1, dn1)
     wait_all(head.stores)
@@ -537,10 +576,10 @@
     s0[...] = dot_nn(s1[...], mg[...]).astype(BF16)
     for n, (src, dst) in enumerate(((s0, s1), (s1, s0))):
         g_copies[3 + n].wait()
-        wide_ups[n].update(16, up_pieces, gb_two, up2, TILE)
+        wide_ups[n].update(16, up_pieces, gb_two, up2)
         if n == 0:
             start_all(wide_downs[1].loads)
-        wide_downs[n].update(16, down_pieces, gb_two, dn2, WIDE)
+        wide_downs[n].update(16, down_pieces, gb_two, dn2)
         if n == 0:
             g_second.start()
         stage_two_block(src, dst, normed_ref, acc, up2, dn2)
@@ -576,14 +615,15 @@
 def run_train(x_now, labels, params):
     return pl.pallas_call(
         train_kernel,
-        out_shape=[jax.ShapeDtypeStruct((rows, WIDE), BF16) for rows in (SHARE_ROWS, CLASS_PAD)],
+        out_shape=[jax.ShapeDtypeStruct((rows, WIDE), BF16) for rows in (SHARE_ROWS, CLASS_PAD)]
+        + f32_outs([(MATRICES * SUBLANES, WIDTH)]),
         in_specs=[ANY_SPEC, pl.BlockSpec(memory_space=pltpu.SMEM)] + [ANY_SPEC] * 6,
-        out_specs=[ANY_SPEC] * 2,
+        out_specs=[ANY_SPEC] * 2 + [VMEM_SPEC],
         scratch_shapes=[vmem((ROWS * 4, WIDTH), BF16), vmem((ROWS * 4, WIDTH), F32)]
         + [vmem(shape, F32) for shape in BUF_SHAPES[:5]] + [vmem(shape, BF16) for shape in W_SHAPES[:5]] + [vmem((CLASS_PAD, WIDE), BF16)]
-        + [act()] * 6 + [act(F32), act(), act(), DMA((9,)), vmem((WIDTH, WIDE), F32), vmem((WIDTH, WIDE), F32)]
+        + [act()] * 6 + [act(F32), act(), act(), DMA((12,)), vmem((WIDTH, WIDE), F32), vmem((WIDTH, WIDE), F32)]
         + [vmem((rows, WIDE), BF16) for rows in (SHARE_ROWS, SHARE_ROWS, N_UNITS * TILE, N_UNITS * WIDTH)]
-        + [vmem((DEVS, SUBLANES, WIDE + CLASS_PAD), BF16), vmem((CLASS_PAD, WIDE), BF16)]
+        + [vmem((DEVS, SUBLANES, WIDE + CLASS_PAD), BF16), vmem((CLASS_PAD, WIDE), BF16), vmem((MATRICES * SUBLANES, WIDTH), F32), vmem((MATRICES, SUBLANES, WIDE), F32)]
         + [DMA((N_UNITS, 6, 2, 2)), DMA((DEVS, 2)), DMA((N_UNITS,))],
         compiler_params=pltpu.CompilerParams(vmem_limit_bytes=VMEM_BYTES, collective_id=0, has_side_effects=True),
         cost_estimate=pl.CostEstimate(flops=30_000_000_000, bytes_accessed=40_000_000, transcendentals=0),
@@ -591,11 +631,11 @@
     )(x_now, labels, *params)
 
 
-def run_next(x_next, params, velocities, sums, head_sum):
+def run_next(x_next, params, velocities, *sums):
     return pl.pallas_call(
         next_kernel,
         out_shape=f32_outs([(IMGS, CLASSES)] + list(W_SHAPES) * 2),
-        in_specs=[ANY_SPEC] * 15,
+        in_specs=[ANY_SPEC] * 15 + [VMEM_SPEC],
         out_specs=[VMEM_SPEC] + [ANY_SPEC] * 12,
         scratch_shapes=[vmem((ROWS * 4, WIDTH), BF16), vmem((ROWS * 4, WIDTH), F32)]
         + [vmem(shape, F32) for shape in W_SHAPES[:5]] * 2
@@ -605,7 +645,7 @@
         compiler_params=pltpu.CompilerParams(vmem_limit_bytes=VMEM_BYTES),
         cost_estimate=pl.CostEstimate(flops=10_000_000_000, bytes_accessed=100_000_000, transcendentals=0),
         name='next_part',
-    )(x_next, *params, *velocities, sums, head_sum)
+    )(x_next, *params, *velocities, *sums)
 
 
 def turn_head(arrays):
@@ -615,8 +655,8 @@
 def solution(mesh):
     def local_step(x_now, labels_now, x_next, *weights):
         params, velocities = turn_head(weights[:6]), turn_head(weights[6:])
-        sums, head_sum = run_train(x_now.reshape(ROWS * 4, WIDTH), labels_now, params)
-        outs = run_next(x_next.reshape(ROWS * 4, WIDTH), params, velocities, sums, head_sum)
+        sums = run_train(x_now.reshape(ROWS * 4, WIDTH), labels_now, params)
+        outs = run_next(x_next.reshape(ROWS * 4, WIDTH), params, velocities, *sums)
         return (outs[0], *turn_head(outs[1:7]), *turn_head(outs[7:]))
 
     split = P('data')

time: 162 us -> 164 us (1.012)
  Pallas kernels: 161 us -> 163 us
where the time goes in v2:
time: 164 us; the launch traced here: 163 us
  Pallas kernels  163 us (99%)
    pallas_call x1, Pallas kernels, run_train(): pl.pallas_call(train_kernel, out_shape=[jax.ShapeDtypeStruct((rows, WIDE)...  122 us
    pallas_call x1, Pallas kernels, run_next(): pl.pallas_call(next_kernel, out_shape=f32_outs([(IMGS, CLASSES)] + list(W...  40.4 us

profile of v2, /device:TPU:0, one launch (start us, length us, event | category | flops | bytes accessed | tf_op | source)
XLA Modules:
  0.0 163.5 jit_solution(15074723206007744228)
XLA Ops:
  0.6 122.3 %train_part.1 = (bf16[9216,512]{1,0:T(8,128)(2,1)}, bf16[1024,512]{1,0:T(8,128)(2,1)}, f32[80,128]{1,0:T(8,128)}) custom-call(bf16[3136,128]{1,0:T(8,128)(2,1)} %bitcast.12, s32[4]{0:T(128)} %labels_ref.1, f32[2,128,512]{2,1,0:T(8,128)} %up1_hbm.3, f32[2,512,128]{2,1,0:T(8,128)} %dn1_hbm.3, f32[512,512]{1,0:T(8,128)} %mg_hbm.3, f32[2,512,2048]{2,1,0:T(8,128)} %up2_hbm.3, ...), custom_call_target="tpu_custom_call" | custom-call | flops 30000001024 | bytes 40000000 | tf_op jit(solution)/shard_map/train_part/pallas_call | solution.py:616
  122.9 40.4 %next_part.1 = (f32[4,1000]{1,0:T(4,128)}, f32[2,128,512]{2,1,0:T(8,128)}, f32[2,512,128]{2,1,0:T(8,128)}, f32[512,512]{1,0:T(8,128)}, f32[2,512,2048]{2,1,0:T(8...) custom-call(bf16[3136,128]{1,0:T(8,128)(2,1)} %bitcast.9, ...), custom_call_target="tpu_custom_call" | custom-call | flops 10000000000 | bytes 100000000 | tf_op jit(solution)/shard_map/next_part/pallas_call | solution.py:635

commit v3 on v2

--- a/solution.py
+++ b/solution.py
@@ -248,12 +248,12 @@
         self.start(unit, phase + 1)
 
 
-def train_kernel(x_hbm, labels_ref, up1_hbm, dn1_hbm, mg_hbm, up2_hbm, dn2_hbm, hd_hbm,
-                 sums_hbm, head_hbm, scale_ref,
-                 x_v, x_f32, st_up1, st_dn1, st_mg, st_up2, st_dn2,
+def train_kernel(x_hbm, x_next_hbm, labels_ref, up1_hbm, dn1_hbm, mg_hbm, up2_hbm, dn2_hbm, hd_hbm,
+                 final, st_up1, st_dn1, st_mg, st_up2, st_dn2, r0, g_hd, scale_ref,
+                 x_v, x_f32,
                  up1, dn1, mg, up2, dn2, hd,
-                 r0, r1, r2, s0, s1, normed_ref, acc, grad_a, grad_b, sems,
-                 du1, dv1, own, final, land1, land2, factors, g_hd, w_sums, g_sums, link_sems, factor_sems, out_sems):
+                 r1, r2, s0, s1, normed_ref, acc, grad_a, grad_b, sems,
+                 du1, dv1, own, land1, land2, factors, w_sums, g_sums, link_sems, factor_sems):
     links = Links(own, final, land1, land2, link_sems)
     me = links.me
     st_hd = st_dn2.at[pl.ds(0, CLASSES)]
@@ -357,17 +357,12 @@
     own[LAST * UNIT:LAST * UNIT + WIDE, :] = dot_tn(r2[...], grad_a[...]).astype(BF16)
     grad_b[...] = dot_nt(grad_a[...], mg[...]).astype(BF16)
 
-    def out_copy(unit):
-        rows = pl.ds(unit * UNIT, UNIT)
-        return pltpu.make_async_copy(final.at[rows], sums_hbm.at[rows], out_sems.at[unit])
-
     def reduced(unit):
         links.reduce_second(unit)
         links.start(unit, SECOND_BACK)
 
     def finish(unit):
         links.wait(unit, PAIR_BACK)
-        out_copy(unit).start()
         start = unit * UNIT
         if unit < LAST:
             for k in range(4):
@@ -382,7 +377,7 @@
         w_sums[pl.ds(matrix * SUBLANES, SUBLANES), :] = jnp.broadcast_to(total_of(square_sum(ref, 0, rows, step)), (SUBLANES, WIDTH))
 
     reloads = [pltpu.make_async_copy(src, dst, sems.at[9 + i]) for i, (src, dst) in enumerate((
-        (up2_hbm.at[0], st_up2), (dn2_hbm.at[0], st_dn2), (dn2_hbm.at[1], st_dn2)))]
+        (up2_hbm.at[0], st_up2), (dn2_hbm.at[1], st_dn2), (x_next_hbm, x_v), (dn2_hbm.at[0], st_dn2)))]
 
     def weigh_small(_):
         for n in range(2):
@@ -392,17 +387,18 @@
         weigh(6, st_up2, WIDE, 16)
         w_hd = square_sum(st_dn2, 0, 992, 32) + square_sum(st_dn2, 992, SUBLANES, SUBLANES)
         w_sums[pl.ds(9 * SUBLANES, SUBLANES), :] = jnp.broadcast_to(total_of(w_hd), (SUBLANES, WIDTH))
-        start_all(reloads[:2])
+        start_all(reloads[:3])
 
     def weigh_first(_):
-        wait_all(reloads[:2])
+        wait_all(reloads[:3])
         weigh(5, st_up2, WIDE, 16)
+        weigh(8, st_dn2, HID_TWO, SHARD)
+        reloads[3].start()
+        permute_tokens(x_v, x_f32, r0)
+
+    def weigh_second(_):
+        reloads[3].wait()
         weigh(7, st_dn2, HID_TWO, SHARD)
-        reloads[2].start()
-
-    def weigh_second(_):
-        reloads[2].wait()
-        weigh(8, st_dn2, HID_TWO, SHARD)
         g_sums[9] = square_sum(g_hd, 0, CLASS_PAD, SHARD)
 
     def back_first(unit):
@@ -462,8 +458,6 @@
     lax.fori_loop(0, half_tiles, head_tile, 0)
     run_all(((links.reduce_pair, LAST), (reduced, 5), (back_first, 3)))
     lax.fori_loop(half_tiles, 2 * half_tiles, head_tile, 0)
-    head_copy = pltpu.make_async_copy(g_hd, head_hbm, factor_sems.at[0, 0])
-    head_copy.start()
     run_all(((reduced, 6), (weigh_small, 0), (first, LAST), (weigh_first, 0), (back_pair, 0), (back_pair, 1), (finish, 0), (weigh_second, 0), (back_pair, 2), (finish, 1), (reduced, 7),
              (reduced, LAST), (back_first, 4), (finish, 2), (back_first, 5), (back_pair, 3), (back_first, 6), (back_first, LAST),
              (finish, 3), (back_pair, 4), (back_first, 7), (back_pair, 5), (finish, 4), (back_pair, LAST), (back_pair, 6), (finish, 5),
@@ -471,9 +465,6 @@
     for matrix in range(MATRICES):
         sl = pl.ds(matrix * SUBLANES, SUBLANES)
         scale_ref[sl, :] = TRUST * (jnp.sqrt(w_sums[sl, :]) / jnp.sqrt(total_of(g_sums[matrix])))
-    for unit in range(N_UNITS):
-        out_copy(unit).wait()
-    head_copy.wait()
 
 
 def lars_matrix(steps, piece, scale, tails=()):
@@ -521,9 +512,9 @@
     def __init__(self, w, v, out_w, out_v, buf_w, buf_v, sems, scales, slot):
         self.buf_w, self.buf_v = buf_w, buf_v
         self.scale = scales.at[pl.ds(slot * SUBLANES, 1), pl.ds(0, 1)]
-        ends = ((w, buf_w), (v, buf_v)), ((buf_w, out_w), (buf_v, out_v))
+        ins = ((v, buf_v),) if w is None else ((v, buf_v), (w, buf_w))
         self.loads, self.stores = ([pltpu.make_async_copy(src, dst, sems.at[slot, k, i]) for i, (src, dst) in enumerate(part)]
-                                   for k, part in enumerate(ends))
+                                   for k, part in enumerate((ins, ((buf_w, out_w), (buf_v, out_v)))))
 
     def update(self, steps, make, grad, cast, *rest, tails=()):
         wait_all(self.loads)
@@ -531,57 +522,43 @@
         start_all(self.stores)
 
 
-def next_kernel(x_hbm, up1_hbm, dn1_hbm, mg_hbm, up2_hbm, dn2_hbm, hd_hbm,
-                vup1_hbm, vdn1_hbm, vmg_hbm, vup2_hbm, vdn2_hbm, vhd_hbm, sums_hbm, ghd_hbm, scales,
+def next_kernel(up2_hbm, dn2_hbm, hd_hbm, vup1_hbm, vdn1_hbm, vmg_hbm, vup2_hbm, vdn2_hbm, vhd_hbm,
+                sums, in_up1, in_dn1, in_mg, in_up2, in_dn2, r0, g_hd, scales,
                 logits_ref, o_up1, o_dn1, o_mg, o_up2, o_dn2, o_hd, ov_up1, ov_dn1, ov_mg, ov_up2, ov_dn2, ov_hd,
-                x_v, x_f32, wb_up1, wb_dn1, wb_mg, wb_up2, wb_dn2, vb_up1, vb_dn1, vb_mg, vb_up2, vb_dn2,
-                gb_small, gb_turn, gb_two, gb_hd, up1, dn1, mg, up2, dn2, hd, r0, s0, s1, normed_ref, acc, sems, sem_g):
-    def pair(n, slot, *refs):
-        return Pair(*(ref.at[n] for ref in refs), sems, scales, slot)
-
-    ups = [pair(n, n, up1_hbm, vup1_hbm, o_up1, ov_up1, wb_up1, vb_up1) for n in range(2)]
-    downs = [pair(n, 2 + n, dn1_hbm, vdn1_hbm, o_dn1, ov_dn1, wb_dn1, vb_dn1) for n in range(2)]
-    merge = Pair(mg_hbm, vmg_hbm, o_mg, ov_mg, wb_mg, vb_mg, sems, scales, 4)
-    wide_ups = [pair(n, 5 + n, up2_hbm, vup2_hbm, o_up2, ov_up2, wb_up2, vb_up2) for n in range(2)]
-    wide_downs = [pair(n, 7 + n, dn2_hbm, vdn2_hbm, o_dn2, ov_dn2, wb_dn2, vb_dn2) for n in range(2)]
-    wb_hd, vb_hd = (buf.at[1, pl.ds(0, CLASSES)] for buf in (wb_dn2, vb_dn2))
+                w_up1, w_dn1, w_mg, w_up2, w_dn2,
+                vb_up1, vb_dn1, vb_mg, vb_up2, vb_dn2, wb_up2, wb_dn2,
+                gb_turn, up1, dn1, mg, up2, dn2, hd, s0, s1, normed_ref, acc, sems):
+    ups = [Pair(None, vup1_hbm.at[n], o_up1.at[n], ov_up1.at[n], w_up1.at[n], vb_up1.at[n], sems, scales, n) for n in range(2)]
+    downs = [Pair(None, vdn1_hbm.at[n], o_dn1.at[n], ov_dn1.at[n], w_dn1.at[n], vb_dn1.at[n], sems, scales, 2 + n) for n in range(2)]
+    merge = Pair(None, vmg_hbm, o_mg, ov_mg, w_mg, vb_mg, sems, scales, 4)
+    wide_ups = [Pair((None, up2_hbm.at[1])[n], vup2_hbm.at[n], o_up2.at[n], ov_up2.at[n], (w_up2, wb_up2)[n], vb_up2.at[n],
+                     sems, scales, 5 + n) for n in range(2)]
+    wide_downs = [Pair((None, dn2_hbm.at[1])[n], vdn2_hbm.at[n], o_dn2.at[n], ov_dn2.at[n], (w_dn2, wb_dn2)[n], vb_dn2.at[n],
+                       sems, scales, 7 + n) for n in range(2)]
+    wb_hd, vb_hd = wb_dn2.at[pl.ds(0, CLASSES)], vb_dn2.at[1, pl.ds(0, CLASSES)]
     head = Pair(hd_hbm, vhd_hbm, o_hd, ov_hd, wb_hd, vb_hd, sems, scales, 9)
-    g_copies = [pltpu.make_async_copy(src, dst, sem_g.at[i]) for i, (src, dst) in enumerate((
-        (x_hbm, x_v), (sums_hbm.at[pl.ds(LAST * UNIT, UNIT)], gb_small), (ghd_hbm, gb_hd),
-        (sums_hbm.at[pl.ds(HELD * UNIT, HELD * UNIT)], gb_two), (sums_hbm.at[pl.ds(0, HELD * UNIT)], gb_two)))]
-    x_copy, g_small, g_head, g_first, g_second = g_copies
-    start_all((x_copy, g_small))
-    for each in ups + downs:
+    for each in ups + downs + [merge, head] + wide_ups[:1]:
         start_all(each.loads)
-    x_copy.wait()
-    start_all(merge.loads)
-    permute_tokens(x_v, x_f32, r0)
-    g_small.wait()
-    g_head.start()
-    start_all(head.loads)
+    small = sums.at[pl.ds(LAST * UNIT, UNIT)]
     for n in range(2):
-        ups[n].update(2, row_pieces, gb_small.at[pl.ds(WIDE + n * WIDTH, WIDTH)], up1.at[n], SHARD)
-        gb_turn[...] = gb_small[pl.ds(WIDE + TILE + n * WIDTH, WIDTH), :].astype(F32).T
+        ups[n].update(2, row_pieces, small.at[pl.ds(WIDE + n * WIDTH, WIDTH)], up1.at[n], SHARD)
+        gb_turn[...] = small[pl.ds(WIDE + TILE + n * WIDTH, WIDTH), :].astype(F32).T
         downs[n].update(4, row_pieces, gb_turn, dn1.at[n], WIDTH)
-    merge.update(8, row_pieces, gb_small.at[pl.ds(0, WIDE)], mg, SHARD)
-    g_first.start()
-    start_all(wide_ups[0].loads)
-    g_head.wait()
+    start_all(wide_downs[0].loads)
+    merge.update(8, row_pieces, small.at[pl.ds(0, WIDE)], mg, SHARD)
     tail = pl.ds(992, SUBLANES)
-    head.update(31, row_pieces, gb_hd, hd, 32, tails=[(wb_hd.at[tail], vb_hd.at[tail], gb_hd.at[tail], hd.at[tail])])
-    start_all(wide_downs[0].loads)
+    head.update(31, row_pieces, g_hd, hd, 32, tails=[(wb_hd.at[tail], vb_hd.at[tail], g_hd.at[tail], hd.at[tail])])
+    start_all(wide_ups[1].loads)
+    wide_ups[0].update(16, up_pieces, sums.at[pl.ds(HELD * UNIT, HELD * UNIT)], up2)
+    wide_downs[0].update(16, down_pieces, sums.at[pl.ds(HELD * UNIT, HELD * UNIT)], dn2)
+    wait_all(head.stores)
+    start_all(wide_downs[1].loads)
     stage_one_forward(r0, s0, s1, up1, dn1)
-    wait_all(head.stores)
-    start_all(wide_ups[1].loads)
     s0[...] = dot_nn(s1[...], mg[...]).astype(BF16)
     for n, (src, dst) in enumerate(((s0, s1), (s1, s0))):
-        g_copies[3 + n].wait()
-        wide_ups[n].update(16, up_pieces, gb_two, up2)
-        if n == 0:
-            start_all(wide_downs[1].loads)
-        wide_downs[n].update(16, down_pieces, gb_two, dn2)
-        if n == 0:
-            g_second.start()
+        if n:
+            wide_ups[n].update(16, up_pieces, sums.at[pl.ds(0, HELD * UNIT)], up2)
+            wide_downs[n].update(16, down_pieces, sums.at[pl.ds(0, HELD * UNIT)], dn2)
         stage_two_block(src, dst, normed_ref, acc, up2, dn2)
     head_b = pooled_norm(s0[...])[0].astype(BF16)
     logits_ref[...] = dot_nt(head_b, hd[...])[:IMGS]
@@ -612,40 +589,45 @@
 DMA = pltpu.SemaphoreType.DMA
 
 
-def run_train(x_now, labels, params):
+HANDED = ((SHARE_ROWS, WIDE), BF16), *((shape, F32) for shape in BUF_SHAPES[:5]), ((ROWS, WIDE), BF16), ((CLASS_PAD, WIDE), BF16)
+HANDED_BYTES = 22_000_000
+
+
+def run_train(x_now, x_next, labels, params):
     return pl.pallas_call(
         train_kernel,
-        out_shape=[jax.ShapeDtypeStruct((rows, WIDE), BF16) for rows in (SHARE_ROWS, CLASS_PAD)]
-        + f32_outs([(MATRICES * SUBLANES, WIDTH)]),
-        in_specs=[ANY_SPEC, pl.BlockSpec(memory_space=pltpu.SMEM)] + [ANY_SPEC] * 6,
-        out_specs=[ANY_SPEC] * 2 + [VMEM_SPEC],
+        out_shape=[vmem(*each) for each in HANDED] + f32_outs([(MATRICES * SUBLANES, WIDTH)]),
+        in_specs=[ANY_SPEC] * 2 + [pl.BlockSpec(memory_space=pltpu.SMEM)] + [ANY_SPEC] * 6,
+        out_specs=[VMEM_SPEC] * 9,
         scratch_shapes=[vmem((ROWS * 4, WIDTH), BF16), vmem((ROWS * 4, WIDTH), F32)]
-        + [vmem(shape, F32) for shape in BUF_SHAPES[:5]] + [vmem(shape, BF16) for shape in W_SHAPES[:5]] + [vmem((CLASS_PAD, WIDE), BF16)]
-        + [act()] * 6 + [act(F32), act(), act(), DMA((12,)), vmem((WIDTH, WIDE), F32), vmem((WIDTH, WIDE), F32)]
-        + [vmem((rows, WIDE), BF16) for rows in (SHARE_ROWS, SHARE_ROWS, N_UNITS * TILE, N_UNITS * WIDTH)]
-        + [vmem((DEVS, SUBLANES, WIDE + CLASS_PAD), BF16), vmem((CLASS_PAD, WIDE), BF16), vmem((MATRICES * SUBLANES, WIDTH), F32), vmem((MATRICES, SUBLANES, WIDE), F32)]
-        + [DMA((N_UNITS, 6, 2, 2)), DMA((DEVS, 2)), DMA((N_UNITS,))],
-        compiler_params=pltpu.CompilerParams(vmem_limit_bytes=VMEM_BYTES, collective_id=0, has_side_effects=True),
+        + [vmem(shape, BF16) for shape in W_SHAPES[:5]] + [vmem((CLASS_PAD, WIDE), BF16)]
+        + [act()] * 5 + [act(F32), act(), act(), DMA((13,)), vmem((WIDTH, WIDE), F32), vmem((WIDTH, WIDE), F32)]
+        + [vmem((rows, WIDE), BF16) for rows in (SHARE_ROWS, N_UNITS * TILE, N_UNITS * WIDTH)]
+        + [vmem((DEVS, SUBLANES, WIDE + CLASS_PAD), BF16), vmem((MATRICES * SUBLANES, WIDTH), F32), vmem((MATRICES, SUBLANES, WIDE), F32)]
+        + [DMA((N_UNITS, 6, 2, 2)), DMA((DEVS, 2))],
+        compiler_params=pltpu.CompilerParams(vmem_limit_bytes=VMEM_BYTES - HANDED_BYTES, collective_id=0, has_side_effects=True),
         cost_estimate=pl.CostEstimate(flops=30_000_000_000, bytes_accessed=40_000_000, transcendentals=0),
         name='train_part',
-    )(x_now, labels, *params)
-
-
-def run_next(x_next, params, velocities, *sums):
-    return pl.pallas_call(
+    )(x_now, x_next, labels, *params)
+
+
+def run_next(params, velocities, handed):
+    held = [vmem(*each) for each in HANDED[1:6]]
+    handed = [pltpu.with_memory_space_constraint(each, pltpu.VMEM) for each in handed[:8]] + list(handed[8:])
+    outs = pl.pallas_call(
         next_kernel,
-        out_shape=f32_outs([(IMGS, CLASSES)] + list(W_SHAPES) * 2),
-        in_specs=[ANY_SPEC] * 15 + [VMEM_SPEC],
-        out_specs=[VMEM_SPEC] + [ANY_SPEC] * 12,
-        scratch_shapes=[vmem((ROWS * 4, WIDTH), BF16), vmem((ROWS * 4, WIDTH), F32)]
-        + [vmem(shape, F32) for shape in W_SHAPES[:5]] * 2
-        + [vmem((UNIT, WIDE), BF16), vmem((WIDE, WIDTH), F32), vmem((HELD * UNIT, WIDE), BF16), vmem((CLASS_PAD, WIDE), BF16)]
+        out_shape=f32_outs([(IMGS, CLASSES)] + list(W_SHAPES) * 2) + held,
+        in_specs=[ANY_SPEC] * 9 + [VMEM_SPEC] * 9,
+        out_specs=[VMEM_SPEC] + [ANY_SPEC] * 12 + [VMEM_SPEC] * 5,
+        scratch_shapes=[vmem(shape, F32) for shape in W_SHAPES[:5] + BUF_SHAPES[3:5]] + [vmem((WIDE, WIDTH), F32)]
         + [vmem(shape, BF16) for shape in BUF_SHAPES]
-        + [act()] * 4 + [act(F32), DMA((10, 2, 2)), DMA((5,))],
-        compiler_params=pltpu.CompilerParams(vmem_limit_bytes=VMEM_BYTES),
+        + [act()] * 3 + [act(F32), DMA((10, 2, 2))],
+        input_output_aliases={10 + i: 13 + i for i in range(5)},
+        compiler_params=pltpu.CompilerParams(vmem_limit_bytes=VMEM_BYTES - HANDED_BYTES),
         cost_estimate=pl.CostEstimate(flops=10_000_000_000, bytes_accessed=100_000_000, transcendentals=0),
         name='next_part',
-    )(x_next, *params, *velocities, *sums)
+    )(*params[3:], *velocities, *handed)
+    return outs[:13]
 
 
 def turn_head(arrays):
@@ -655,8 +637,8 @@
 def solution(mesh):
     def local_step(x_now, labels_now, x_next, *weights):
         params, velocities = turn_head(weights[:6]), turn_head(weights[6:])
-        sums = run_train(x_now.reshape(ROWS * 4, WIDTH), labels_now, params)
-        outs = run_next(x_next.reshape(ROWS * 4, WIDTH), params, velocities, *sums)
+        handed = run_train(x_now.reshape(ROWS * 4, WIDTH), x_next.reshape(ROWS * 4, WIDTH), labels_now, params)
+        outs = run_next(params, velocities, handed)
         return (outs[0], *turn_head(outs[1:7]), *turn_head(outs[7:]))
 
     split = P('data')

time: 164 us -> 157 us (0.957)
  Pallas kernels: 163 us -> 156 us
    pallas_call x1, Pallas kernels: 40.4 us -> 34.8 us  [run_next(): pl.pallas_call(next_kernel, out_shape=f32_outs([(IMGS, CLASSES)] + list(W...]
where the time goes in v3:
time: 157 us
  Pallas kernels  156 us (99%)
    pallas_call x1, Pallas kernels, run_train(): pl.pallas_call(train_kernel, out_shape=[vmem(*each) for each in HANDED] +...  122 us
    pallas_call x1, Pallas kernels, run_next(): pl.pallas_call(next_kernel, out_shape=f32_outs([(IMGS, CLASSES)] + list(W...  34.8 us

profile of v3, /device:TPU:0, one launch (start us, length us, event | category | flops | bytes accessed | tf_op | source)
XLA Modules:
  0.0 157.2 jit_solution(9510707595320925799)
XLA Ops:
  0.6 121.6 %train_part.1 = (bf16[9216,512]{1,0:T(8,128)(2,1)S(1)}, f32[2,128,512]{2,1,0:T(8,128)S(1)}, f32[2,512,128]{2,1,0:T(8,128)S(1)}, f32[512,512]{1,0:T(8,128)S(1)}, ...) custom-call(bf16[3136,128]{1,0:T(8,128)(2,1)} %bitcast.11, ...), custom_call_target="tpu_custom_call" | custom-call | flops 30000001024 | bytes 40000000 | tf_op jit(solution)/shard_map/train_part/pallas_call | solution.py:597
  122.2 34.8 %next_part.1 = (f32[4,1000]{1,0:T(4,128)}, f32[2,128,512]{2,1,0:T(8,128)}, f32[2,512,128]{2,1,0:T(8,128)}, f32[512,512]{1,0:T(8,128)}, f32[2,512,2048]{2,1,0:T(8...) custom-call(f32[2,512,2048]{2,1,0:T(8,128)} %up2_hbm.3, ...), custom_call_target="tpu_custom_call", output_to_operand_aliasing={{13}: (10, {}), {14}: (11, {}), {15}: (12, {}), {16}: (13, ... | custom-call | flops 10000000000 | bytes 100000000 | tf_op jit(solution)/shard_map/next_part/pallas_call | solution.py:617

commit v4 on v3

--- a/solution.py
+++ b/solution.py
@@ -87,8 +87,10 @@
     return (res_f + dot_nn(act, w_down)).astype(BF16)
 
 
-def stage_one_forward(r0, r1, r2, up_one, down_one):
+def stage_one_forward(r0, r1, r2, up_one, down_one, slots=()):
     def body(j, carry):
+        for k, steps in enumerate(slots):
+            pl.when(j == k)(lambda steps=steps: run_all(steps))
         sl = lanes(j, WIDTH)
         mid = stage_one_block(r0[:, sl], up_one[0], down_one[0])
         r1[:, sl] = mid
@@ -133,6 +135,7 @@
 LAST = N_UNITS - 1
 HELD = 4
 MATRICES = 10
+SENT = 5
 PAIR_OUT, FIRST_OUT, SECOND_OUT, SECOND_BACK, FIRST_BACK, PAIR_BACK = range(6)
 
 
@@ -160,6 +163,11 @@
 
 def total_of(tile):
     return jnp.sum(jnp.sum(tile, axis=0, keepdims=True), axis=1, keepdims=True)
+
+
+def run_all(steps):
+    for action, unit in steps:
+        action(unit)
 
 
 class Links:
@@ -243,17 +251,23 @@
             land = pl.ds(pl.multiple_of(unit * WIDTH + lane * SHARD, SHARD), SHARD)
             self.final[sl, :] = self.own[sl, :] + self.land2[land, :]
 
+    def back_first(self, unit):
+        self.forward(unit, SECOND_BACK)
+
+    def back_pair(self, unit):
+        self.forward(unit, FIRST_BACK)
+
     def forward(self, unit, phase):
         self.wait(unit, phase)
         self.start(unit, phase + 1)
 
 
-def train_kernel(x_hbm, x_next_hbm, labels_ref, up1_hbm, dn1_hbm, mg_hbm, up2_hbm, dn2_hbm, hd_hbm,
-                 final, st_up1, st_dn1, st_mg, st_up2, st_dn2, r0, g_hd, scale_ref,
-                 x_v, x_f32,
+def train_kernel(x_hbm, labels_ref, up1_hbm, dn1_hbm, mg_hbm, up2_hbm, dn2_hbm, hd_hbm,
+                 final, g_hd,
+                 x_v, x_f32, st_up1, st_dn1, st_mg, st_up2, st_dn2, r0,
                  up1, dn1, mg, up2, dn2, hd,
                  r1, r2, s0, s1, normed_ref, acc, grad_a, grad_b, sems,
-                 du1, dv1, own, land1, land2, factors, w_sums, g_sums, link_sems, factor_sems):
+                 du1, dv1, own, land1, land2, factors, link_sems, factor_sems):
     links = Links(own, final, land1, land2, link_sems)
     me = links.me
     st_hd = st_dn2.at[pl.ds(0, CLASSES)]
@@ -361,61 +375,10 @@
         links.reduce_second(unit)
         links.start(unit, SECOND_BACK)
 
-    def finish(unit):
-        links.wait(unit, PAIR_BACK)
-        start = unit * UNIT
-        if unit < LAST:
-            for k in range(4):
-                matrix = (6 if unit < HELD else 5) + 2 * (k % 2)
-                g_sums[matrix] += square_sum(final, start + k * TILE, TILE, SHARD)
-        else:
-            g_sums[4] = square_sum(final, start, WIDE, SHARD)
-            for k in range(4):
-                g_sums[k] = square_sum(final, start + WIDE + k * WIDTH, WIDTH, SHARD)
-
-    def weigh(matrix, ref, rows, step):
-        w_sums[pl.ds(matrix * SUBLANES, SUBLANES), :] = jnp.broadcast_to(total_of(square_sum(ref, 0, rows, step)), (SUBLANES, WIDTH))
-
-    reloads = [pltpu.make_async_copy(src, dst, sems.at[9 + i]) for i, (src, dst) in enumerate((
-        (up2_hbm.at[0], st_up2), (dn2_hbm.at[1], st_dn2), (x_next_hbm, x_v), (dn2_hbm.at[0], st_dn2)))]
-
-    def weigh_small(_):
-        for n in range(2):
-            weigh(n, st_up1.at[n], WIDTH, SHARD)
-            weigh(2 + n, st_dn1.at[n], WIDE, WIDTH)
-        weigh(4, st_mg, WIDE, SHARD)
-        weigh(6, st_up2, WIDE, 16)
-        w_hd = square_sum(st_dn2, 0, 992, 32) + square_sum(st_dn2, 992, SUBLANES, SUBLANES)
-        w_sums[pl.ds(9 * SUBLANES, SUBLANES), :] = jnp.broadcast_to(total_of(w_hd), (SUBLANES, WIDTH))
-        start_all(reloads[:3])
-
-    def weigh_first(_):
-        wait_all(reloads[:3])
-        weigh(5, st_up2, WIDE, 16)
-        weigh(8, st_dn2, HID_TWO, SHARD)
-        reloads[3].start()
-        permute_tokens(x_v, x_f32, r0)
-
-    def weigh_second(_):
-        reloads[3].wait()
-        weigh(7, st_dn2, HID_TWO, SHARD)
-        g_sums[9] = square_sum(g_hd, 0, CLASS_PAD, SHARD)
-
-    def back_first(unit):
-        links.forward(unit, SECOND_BACK)
-
-    def back_pair(unit):
-        links.forward(unit, FIRST_BACK)
-
-    def run_all(steps):
-        for action, unit in steps:
-            action(unit)
-
-    g_sums[...] = jnp.zeros_like(g_sums)
     links.reduce_pair(7)
     first = links.reduce_first
-    slots = {1: (((reduced, 0), (reduced, 1), (reduced, 2), (first, 4)), ((first, 5),), ((reduced, 3),), ((first, 6), (back_first, 0))),
-             0: (((back_first, 1),), ((back_first, 2),), ((reduced, 4),), ((first, 7),))}
+    slots = {1: (((reduced, 0), (reduced, 1), (reduced, 2), (first, 4)), ((first, 5),), ((reduced, 3),), ((first, 6),)),
+             0: ((), (), ((reduced, 4),), ((first, 7),))}
 
     for n, src, g_in, g_out in ((1, r1, grad_b, grad_a), (0, r0, grad_a, grad_b)):
         du1[...] = jnp.zeros_like(du1)
@@ -456,15 +419,12 @@
         return carry
     half_tiles = CLASS_PAD // WIDTH // 2
     lax.fori_loop(0, half_tiles, head_tile, 0)
-    run_all(((links.reduce_pair, LAST), (reduced, 5), (back_first, 3)))
+    run_all(((links.reduce_pair, LAST), (links.reduce_second, 5)))
     lax.fori_loop(half_tiles, 2 * half_tiles, head_tile, 0)
-    run_all(((reduced, 6), (weigh_small, 0), (first, LAST), (weigh_first, 0), (back_pair, 0), (back_pair, 1), (finish, 0), (weigh_second, 0), (back_pair, 2), (finish, 1), (reduced, 7),
-             (reduced, LAST), (back_first, 4), (finish, 2), (back_first, 5), (back_pair, 3), (back_first, 6), (back_first, LAST),
-             (finish, 3), (back_pair, 4), (back_first, 7), (back_pair, 5), (finish, 4), (back_pair, LAST), (back_pair, 6), (finish, 5),
-             (finish, LAST), (back_pair, 7), (finish, 6), (finish, 7)))
-    for matrix in range(MATRICES):
-        sl = pl.ds(matrix * SUBLANES, SUBLANES)
-        scale_ref[sl, :] = TRUST * (jnp.sqrt(w_sums[sl, :]) / jnp.sqrt(total_of(g_sums[matrix])))
+    run_all(((links.reduce_second, 6), (first, LAST)))
+    for unit in range(SENT):
+        links.wait(unit, SECOND_BACK)
+    run_all(((links.reduce_second, 7), (links.reduce_second, LAST)))
 
 
 def lars_matrix(steps, piece, scale, tails=()):
@@ -512,7 +472,7 @@
     def __init__(self, w, v, out_w, out_v, buf_w, buf_v, sems, scales, slot):
         self.buf_w, self.buf_v = buf_w, buf_v
         self.scale = scales.at[pl.ds(slot * SUBLANES, 1), pl.ds(0, 1)]
-        ins = ((v, buf_v),) if w is None else ((v, buf_v), (w, buf_w))
+        ins = () if w is None else ((v, buf_v), (w, buf_w))
         self.loads, self.stores = ([pltpu.make_async_copy(src, dst, sems.at[slot, k, i]) for i, (src, dst) in enumerate(part)]
                                    for k, part in enumerate((ins, ((buf_w, out_w), (buf_v, out_v)))))
 
@@ -522,47 +482,105 @@
         start_all(self.stores)
 
 
-def next_kernel(up2_hbm, dn2_hbm, hd_hbm, vup1_hbm, vdn1_hbm, vmg_hbm, vup2_hbm, vdn2_hbm, vhd_hbm,
-                sums, in_up1, in_dn1, in_mg, in_up2, in_dn2, r0, g_hd, scales,
+def gather_kernel(in_final, x_hbm, up1_hbm, dn1_hbm, mg_hbm, up2_hbm, dn2_hbm, vup1_hbm, vdn1_hbm, vmg_hbm, vup2_hbm, vdn2_hbm, g_hd, hd_hbm,
+                  final, w_up1, w_dn1, w_mg, w_up2, w_dn2, v_up1, v_dn1, v_mg, v_up2, v_dn2, mid, scale_ref,
+                  x_v, x_f32, r0, s1, up1, dn1, mg, gb_turn, st_hd, w_sums, g_sums, link_sems, sems):
+    links = Links(None, final, None, None, link_sems)
+    barrier = pltpu.get_barrier_semaphore()
+    peers = (links.pair, links.x_peer, links.y_peer)
+    for peer in peers:
+        pl.semaphore_signal(barrier, inc=1, device_id=(peer,), device_id_type=pl.DeviceIdType.MESH)
+    copies = [pltpu.make_async_copy(src, dst, sems.at[i]) for i, (src, dst) in enumerate((
+        (x_hbm, x_v), (up1_hbm, w_up1), (dn1_hbm, w_dn1), (mg_hbm, w_mg), (vup1_hbm, v_up1), (vdn1_hbm, v_dn1), (vmg_hbm, v_mg),
+        (up2_hbm, w_up2), (dn2_hbm, w_dn2), (hd_hbm, st_hd), (vup2_hbm, v_up2), (vdn2_hbm, v_dn2)))]
+    start_all(copies[:7])
+    pl.semaphore_wait(barrier, len(peers))
+    links.start(LAST, SECOND_BACK)
+    links.start(4, FIRST_BACK)
+    g_sums[...] = jnp.zeros_like(g_sums)
+
+    def finish(unit):
+        links.wait(unit, PAIR_BACK)
+        start = unit * UNIT
+        if unit < LAST:
+            for k in range(4):
+                matrix = (6 if unit < HELD else 5) + 2 * (k % 2)
+                g_sums[matrix] += square_sum(final, start + k * TILE, TILE, SHARD)
+        else:
+            g_sums[4] = square_sum(final, start, WIDE, SHARD)
+            for k in range(4):
+                g_sums[k] = square_sum(final, start + WIDE + k * WIDTH, WIDTH, SHARD)
+
+    def weigh(matrix, total):
+        w_sums[pl.ds(matrix * SUBLANES, SUBLANES), :] = jnp.broadcast_to(total_of(total), (SUBLANES, WIDTH))
+
+    def scale_matrix(matrix):
+        sl = pl.ds(matrix * SUBLANES, SUBLANES)
+        scale = TRUST * (jnp.sqrt(w_sums[sl, :]) / jnp.sqrt(total_of(g_sums[matrix])))
+        scale_ref[sl, :] = scale
+        return scale[:1, :1]
+
+    copies[0].wait()
+    start_all(copies[7:])
+    permute_tokens(x_v, x_f32, r0)
+    wait_all(copies[1:7])
+    for n in range(2):
+        weigh(n, square_sum(w_up1.at[n], 0, WIDTH, SHARD))
+        weigh(2 + n, square_sum(w_dn1.at[n], 0, WIDE, WIDTH))
+    weigh(4, square_sum(w_mg, 0, WIDE, SHARD))
+    links.back_first(LAST)
+    for unit in range(SENT, LAST):
+        links.start(unit, SECOND_BACK)
+    run_all(((links.back_pair, 4), (links.back_pair, LAST), (links.back_first, 5), (finish, LAST), (links.back_first, 6)))
+    small = final.at[pl.ds(LAST * UNIT, UNIT)]
+    for n in range(2):
+        grad = small.at[pl.ds(WIDE + n * WIDTH, WIDTH)]
+        lars_matrix(2, row_pieces(w_up1.at[n], v_up1.at[n], grad, up1.at[n], SHARD), scale_matrix(n))
+        gb_turn[...] = small[pl.ds(WIDE + TILE + n * WIDTH, WIDTH), :].astype(F32).T
+        lars_matrix(4, row_pieces(w_dn1.at[n], v_dn1.at[n], gb_turn, dn1.at[n], WIDTH), scale_matrix(2 + n))
+    lars_matrix(8, row_pieces(w_mg, v_mg, small.at[pl.ds(0, WIDE)], mg, SHARD), scale_matrix(4))
+    links.back_first(7)
+    for unit in range(HELD):
+        links.start(unit, FIRST_BACK)
+    stage_one_forward(r0, mid, s1, up1, dn1, slots=((), ((links.back_pair, 5), (finish, 4)), ((links.back_pair, 6),), ((links.back_pair, 7), (finish, 5))))
+    mid[...] = dot_nn(s1[...], mg[...]).astype(BF16)
+    wait_all(copies[7:])
+    run_all(((finish, 6), (links.back_pair, 0), (finish, 7)))
+    for n in range(2):
+        weigh(5 + n, square_sum(w_up2.at[n], 0, WIDE, 16))
+        weigh(7 + n, square_sum(w_dn2.at[n], 0, HID_TWO, SHARD))
+        scale_matrix(5) if n else None
+        links.back_pair(1 + n)
+    weigh(9, square_sum(st_hd, 0, 992, 32) + square_sum(st_hd, 992, SUBLANES, SUBLANES))
+    g_sums[9] = square_sum(g_hd, 0, CLASS_PAD, SHARD)
+    run_all(((finish, 0), (links.back_pair, 3), (finish, 1), (finish, 2), (finish, 3)))
+    for matrix in range(6, MATRICES):
+        scale_matrix(matrix)
+
+
+def next_kernel(hd_hbm, vhd_hbm, sums, g_hd, mid, scales, w_up1, w_dn1, w_mg, v_up1, v_dn1, v_mg, in_wu, in_wd, in_vu, in_vd,
                 logits_ref, o_up1, o_dn1, o_mg, o_up2, o_dn2, o_hd, ov_up1, ov_dn1, ov_mg, ov_up2, ov_dn2, ov_hd,
-                w_up1, w_dn1, w_mg, w_up2, w_dn2,
-                vb_up1, vb_dn1, vb_mg, vb_up2, vb_dn2, wb_up2, wb_dn2,
-                gb_turn, up1, dn1, mg, up2, dn2, hd, s0, s1, normed_ref, acc, sems):
-    ups = [Pair(None, vup1_hbm.at[n], o_up1.at[n], ov_up1.at[n], w_up1.at[n], vb_up1.at[n], sems, scales, n) for n in range(2)]
-    downs = [Pair(None, vdn1_hbm.at[n], o_dn1.at[n], ov_dn1.at[n], w_dn1.at[n], vb_dn1.at[n], sems, scales, 2 + n) for n in range(2)]
-    merge = Pair(None, vmg_hbm, o_mg, ov_mg, w_mg, vb_mg, sems, scales, 4)
-    wide_ups = [Pair((None, up2_hbm.at[1])[n], vup2_hbm.at[n], o_up2.at[n], ov_up2.at[n], (w_up2, wb_up2)[n], vb_up2.at[n],
-                     sems, scales, 5 + n) for n in range(2)]
-    wide_downs = [Pair((None, dn2_hbm.at[1])[n], vdn2_hbm.at[n], o_dn2.at[n], ov_dn2.at[n], (w_dn2, wb_dn2)[n], vb_dn2.at[n],
-                       sems, scales, 7 + n) for n in range(2)]
-    wb_hd, vb_hd = wb_dn2.at[pl.ds(0, CLASSES)], vb_dn2.at[1, pl.ds(0, CLASSES)]
+                w_up2, w_dn2, v_up2, v_dn2,
+                wb_hd, vb_hd, up2, dn2, hd, s1, normed_ref, acc, sems, small_sems):
+    wide_ups = [Pair(None, None, o_up2.at[n], ov_up2.at[n], w_up2.at[n], v_up2.at[n], sems, scales, 5 + n) for n in range(2)]
+    wide_downs = [Pair(None, None, o_dn2.at[n], ov_dn2.at[n], w_dn2.at[n], v_dn2.at[n], sems, scales, 7 + n) for n in range(2)]
     head = Pair(hd_hbm, vhd_hbm, o_hd, ov_hd, wb_hd, vb_hd, sems, scales, 9)
-    for each in ups + downs + [merge, head] + wide_ups[:1]:
-        start_all(each.loads)
-    small = sums.at[pl.ds(LAST * UNIT, UNIT)]
-    for n in range(2):
-        ups[n].update(2, row_pieces, small.at[pl.ds(WIDE + n * WIDTH, WIDTH)], up1.at[n], SHARD)
-        gb_turn[...] = small[pl.ds(WIDE + TILE + n * WIDTH, WIDTH), :].astype(F32).T
-        downs[n].update(4, row_pieces, gb_turn, dn1.at[n], WIDTH)
-    start_all(wide_downs[0].loads)
-    merge.update(8, row_pieces, small.at[pl.ds(0, WIDE)], mg, SHARD)
-    tail = pl.ds(992, SUBLANES)
-    head.update(31, row_pieces, g_hd, hd, 32, tails=[(wb_hd.at[tail], vb_hd.at[tail], g_hd.at[tail], hd.at[tail])])
-    start_all(wide_ups[1].loads)
-    wide_ups[0].update(16, up_pieces, sums.at[pl.ds(HELD * UNIT, HELD * UNIT)], up2)
-    wide_downs[0].update(16, down_pieces, sums.at[pl.ds(HELD * UNIT, HELD * UNIT)], dn2)
-    wait_all(head.stores)
-    start_all(wide_downs[1].loads)
-    stage_one_forward(r0, s0, s1, up1, dn1)
-    s0[...] = dot_nn(s1[...], mg[...]).astype(BF16)
-    for n, (src, dst) in enumerate(((s0, s1), (s1, s0))):
-        if n:
-            wide_ups[n].update(16, up_pieces, sums.at[pl.ds(0, HELD * UNIT)], up2)
-            wide_downs[n].update(16, down_pieces, sums.at[pl.ds(0, HELD * UNIT)], dn2)
+    start_all(head.loads)
+    done = [pltpu.make_async_copy(src, dst, small_sems.at[i]) for i, (src, dst) in enumerate((
+        (w_up1, o_up1), (w_dn1, o_dn1), (w_mg, o_mg), (v_up1, ov_up1), (v_dn1, ov_dn1), (v_mg, ov_mg)))]
+    start_all(done)
+    for n, (src, dst) in enumerate(((mid, s1), (s1, s1))):
+        grads = sums.at[pl.ds((1 - n) * HELD * UNIT, HELD * UNIT)]
+        wide_ups[n].update(16, up_pieces, grads, up2)
+        wide_downs[n].update(16, down_pieces, grads, dn2)
+        if n == 0:
+            tail = pl.ds(992, SUBLANES)
+            head.update(31, row_pieces, g_hd, hd, 32, tails=[(wb_hd.at[tail], vb_hd.at[tail], g_hd.at[tail], hd.at[tail])])
         stage_two_block(src, dst, normed_ref, acc, up2, dn2)
-    head_b = pooled_norm(s0[...])[0].astype(BF16)
+    head_b = pooled_norm(s1[...])[0].astype(BF16)
     logits_ref[...] = dot_nt(head_b, hd[...])[:IMGS]
-    for each in ups + downs + [merge] + wide_ups + wide_downs:
+    wait_all(done)
+    for each in [head] + wide_ups + wide_downs:
         wait_all(each.stores)
 
 
@@ -589,44 +607,71 @@
 DMA = pltpu.SemaphoreType.DMA
 
 
-HANDED = ((SHARE_ROWS, WIDE), BF16), *((shape, F32) for shape in BUF_SHAPES[:5]), ((ROWS, WIDE), BF16), ((CLASS_PAD, WIDE), BF16)
-HANDED_BYTES = 22_000_000
-
-
-def run_train(x_now, x_next, labels, params):
+SUMS = (SHARE_ROWS, WIDE), BF16
+HEAD_SUM = (CLASS_PAD, WIDE), BF16
+ROW_BLOCK = (ROWS, WIDE), BF16
+WEIGHTS = tuple((shape, F32) for shape in W_SHAPES[:5])
+
+
+def keep(arrays):
+    return [pltpu.with_memory_space_constraint(each, pltpu.VMEM) for each in arrays]
+
+
+def run_train(x_now, labels, params):
     return pl.pallas_call(
         train_kernel,
-        out_shape=[vmem(*each) for each in HANDED] + f32_outs([(MATRICES * SUBLANES, WIDTH)]),
-        in_specs=[ANY_SPEC] * 2 + [pl.BlockSpec(memory_space=pltpu.SMEM)] + [ANY_SPEC] * 6,
-        out_specs=[VMEM_SPEC] * 9,
+        out_shape=[vmem(*SUMS), vmem(*HEAD_SUM)],
+        in_specs=[ANY_SPEC] + [pl.BlockSpec(memory_space=pltpu.SMEM)] + [ANY_SPEC] * 6,
+        out_specs=[VMEM_SPEC] * 2,
         scratch_shapes=[vmem((ROWS * 4, WIDTH), BF16), vmem((ROWS * 4, WIDTH), F32)]
+        + [vmem(shape, F32) for shape in BUF_SHAPES[:5]] + [act()]
         + [vmem(shape, BF16) for shape in W_SHAPES[:5]] + [vmem((CLASS_PAD, WIDE), BF16)]
-        + [act()] * 5 + [act(F32), act(), act(), DMA((13,)), vmem((WIDTH, WIDE), F32), vmem((WIDTH, WIDE), F32)]
+        + [act()] * 5 + [act(F32), act(), act(), DMA((9,)), vmem((WIDTH, WIDE), F32), vmem((WIDTH, WIDE), F32)]
         + [vmem((rows, WIDE), BF16) for rows in (SHARE_ROWS, N_UNITS * TILE, N_UNITS * WIDTH)]
-        + [vmem((DEVS, SUBLANES, WIDE + CLASS_PAD), BF16), vmem((MATRICES * SUBLANES, WIDTH), F32), vmem((MATRICES, SUBLANES, WIDE), F32)]
+        + [vmem((DEVS, SUBLANES, WIDE + CLASS_PAD), BF16)]
         + [DMA((N_UNITS, 6, 2, 2)), DMA((DEVS, 2))],
-        compiler_params=pltpu.CompilerParams(vmem_limit_bytes=VMEM_BYTES - HANDED_BYTES, collective_id=0, has_side_effects=True),
+        compiler_params=pltpu.CompilerParams(vmem_limit_bytes=VMEM_BYTES - 11_000_000, collective_id=0, has_side_effects=True),
         cost_estimate=pl.CostEstimate(flops=30_000_000_000, bytes_accessed=40_000_000, transcendentals=0),
         name='train_part',
-    )(x_now, x_next, labels, *params)
-
-
-def run_next(params, velocities, handed):
-    held = [vmem(*each) for each in HANDED[1:6]]
-    handed = [pltpu.with_memory_space_constraint(each, pltpu.VMEM) for each in handed[:8]] + list(handed[8:])
+    )(x_now, labels, *params)
+
+
+def run_gather(sums, head_sum, x_next, params, velocities):
+    sums, head_sum = keep((sums, head_sum))
+    return pl.pallas_call(
+        gather_kernel,
+        out_shape=[vmem(*each) for each in (SUMS, *WEIGHTS, *WEIGHTS, ROW_BLOCK)] + f32_outs([(MATRICES * SUBLANES, WIDTH)]),
+        in_specs=[VMEM_SPEC] + [ANY_SPEC] * 11 + [VMEM_SPEC, ANY_SPEC],
+        out_specs=[VMEM_SPEC] * 13,
+        scratch_shapes=[vmem((ROWS * 4, WIDTH), BF16), vmem((ROWS * 4, WIDTH), F32), act(), act()]
+        + [vmem(shape, BF16) for shape in BUF_SHAPES[:3]] + [vmem((WIDE, WIDTH), F32), vmem((CLASSES, WIDE), F32)]
+        + [vmem((MATRICES * SUBLANES, WIDTH), F32), vmem((MATRICES, SUBLANES, WIDE), F32), DMA((N_UNITS, 6, 2, 2)), DMA((12,))],
+        input_output_aliases={0: 0},
+        compiler_params=pltpu.CompilerParams(vmem_limit_bytes=GATHER_BYTES, collective_id=1, has_side_effects=True),
+        cost_estimate=pl.CostEstimate(flops=10_000_000_000, bytes_accessed=40_000_000, transcendentals=0),
+        name='gather_part',
+    )(sums, x_next, *params[:5], *velocities[:5], head_sum, params[5])
+
+
+GATHER_BYTES = 17_000_000
+NEXT_BYTES = 17_500_000
+
+
+def run_next(head, vel_head, head_sum, gathered):
+    sums, w_up1, w_dn1, w_mg, w_up2, w_dn2, v_up1, v_dn1, v_mg, v_up2, v_dn2, mid, scales = gathered
+    held = keep((w_up2, w_dn2, v_up2, v_dn2))
     outs = pl.pallas_call(
         next_kernel,
-        out_shape=f32_outs([(IMGS, CLASSES)] + list(W_SHAPES) * 2) + held,
-        in_specs=[ANY_SPEC] * 9 + [VMEM_SPEC] * 9,
-        out_specs=[VMEM_SPEC] + [ANY_SPEC] * 12 + [VMEM_SPEC] * 5,
-        scratch_shapes=[vmem(shape, F32) for shape in W_SHAPES[:5] + BUF_SHAPES[3:5]] + [vmem((WIDE, WIDTH), F32)]
-        + [vmem(shape, BF16) for shape in BUF_SHAPES]
-        + [act()] * 3 + [act(F32), DMA((10, 2, 2))],
-        input_output_aliases={10 + i: 13 + i for i in range(5)},
-        compiler_params=pltpu.CompilerParams(vmem_limit_bytes=VMEM_BYTES - HANDED_BYTES),
-        cost_estimate=pl.CostEstimate(flops=10_000_000_000, bytes_accessed=100_000_000, transcendentals=0),
+        out_shape=f32_outs([(IMGS, CLASSES)] + list(W_SHAPES) * 2) + [vmem(*each) for each in WEIGHTS[3:] * 2],
+        in_specs=[ANY_SPEC] * 2 + [VMEM_SPEC] * 14,
+        out_specs=[VMEM_SPEC] + [ANY_SPEC] * 12 + [VMEM_SPEC] * 4,
+        scratch_shapes=[vmem((CLASSES, WIDE), F32)] * 2 + [vmem(shape, BF16) for shape in BUF_SHAPES[3:]]
+        + [act()] * 2 + [act(F32), DMA((10, 2, 2)), DMA((6,))],
+        input_output_aliases={12 + i: 13 + i for i in range(4)},
+        compiler_params=pltpu.CompilerParams(vmem_limit_bytes=NEXT_BYTES),
+        cost_estimate=pl.CostEstimate(flops=10_000_000_000, bytes_accessed=50_000_000, transcendentals=0),
         name='next_part',
-    )(*params[3:], *velocities, *handed)
+    )(head, vel_head, *keep((sums, head_sum, mid)), scales, *keep((w_up1, w_dn1, w_mg, v_up1, v_dn1, v_mg)), *held)
     return outs[:13]
 
 
@@ -637,8 +682,9 @@
 def solution(mesh):
     def local_step(x_now, labels_now, x_next, *weights):
         params, velocities = turn_head(weights[:6]), turn_head(weights[6:])
-        handed = run_train(x_now.reshape(ROWS * 4, WIDTH), x_next.reshape(ROWS * 4, WIDTH), labels_now, params)
-        outs = run_next(params, velocities, handed)
+        sums, head_sum = run_train(x_now.reshape(ROWS * 4, WIDTH), labels_now, params)
+        gathered = run_gather(sums, head_sum, x_next.reshape(ROWS * 4, WIDTH), params, velocities)
+        outs = run_next(params[5], velocities[5], head_sum, gathered)
         return (outs[0], *turn_head(outs[1:7]), *turn_head(outs[7:]))
 
     split = P('data')

time: 157 us -> 209 us (1.33)
  local copies, waits for them, and re-layouts: 0 us -> 56.9 us
  Pallas kernels: 156 us -> 151 us
    unnamed x0 -> x54, local copies, waits for them, and re-layouts: none -> 56.9 us
    pallas_call x1, Pallas kernels: 34.8 us -> 23.4 us  [run_next(): pl.pallas_call(next_kernel, out_shape=f32_outs([(IMGS, CLASSES)] + list(W...]
    pallas_call x1 -> x2, Pallas kernels: 122 us -> 127 us  [the longest x1 89.8 us: run_train(): pl.pallas_call(train_kernel, out_shape=[vmem(*SUMS), vmem(*HEAD_SUM)], in...]
where the time goes in v4:
time: 209 us; the launch traced here: 208 us
  Pallas kernels  151 us (72%)
  local copies, waits for them, and re-layouts  56.9 us (27%)
    pallas_call x1, Pallas kernels, run_train(): pl.pallas_call(train_kernel, out_shape=[vmem(*SUMS), vmem(*HEAD_SUM)], in...  89.8 us
    unnamed x54, local copies, waits for them, and re-layouts  56.9 us
    pallas_call x1, Pallas kernels, run_gather(): pl.pallas_call(gather_kernel, out_shape=[vmem(*each) for each in (SUMS, *...  37.3 us
    pallas_call x1, Pallas kernels, run_next(): pl.pallas_call(next_kernel, out_shape=f32_outs([(IMGS, CLASSES)] + list(W...  23.4 us

profile of v4, /device:TPU:0, one launch (start us, length us, event | category | flops | bytes accessed | tf_op | source)
XLA Modules:
  0.0 208.3 jit_solution(2145322978241297993)
XLA Ops:
  0.6 89.8 %train_part.1 = (bf16[9216,512]{1,0:T(8,128)(2,1)S(1)}, bf16[1024,512]{1,0:T(8,128)(2,1)S(1)}) custom-call(bf16[3136,128]{1,0:T(8,128)(2,1)} %bitcast.13, s32[4]{0:T(128)} %labels_ref.1, f32[2,128,512]{2,1,0:T(8,128)} %up1_hbm.3, f32[2,512,128]{2,1,0:T(8,128)} %dn1_hbm.3, f32[512,512]{1,0:T(8,128)} %mg_hbm.3, f32[2,512,2048]{2,1,0:T(8,128)} %up2_hbm.3, ...), custom_call_target="tpu_custom_call" | custom-call | flops 30000001024 | bytes 40000000 | tf_op jit(solution)/shard_map/train_part/pallas_call | solution.py:621
  90.5 0.0 copy-start
  90.5 3.7 %copy-done = bf16[9216,512]{1,0:T(8,128)(2,1)} copy-done((bf16[9216,512]{1,0:T(8,128)(2,1)}, bf16[9216,512]{1,0:T(8,128)(2,1)S(1)}, u32[]{:S(2)}) %copy-start) | copy-done | bytes 9437208
  94.2 0.0 copy-start.12
  94.2 1.0 copy-done.12
  95.1 0.0 copy-start.1
  95.1 3.7 %copy-done.1 = bf16[9216,512]{1,0:T(8,128)(2,1)S(1)} copy-done((bf16[9216,512]{1,0:T(8,128)(2,1)S(1)}, bf16[9216,512]{1,0:T(8,128)(2,1)}, u32[]{:S(2)}) %copy-start.1) | copy-done | bytes 9437208
  98.8 0.0 copy-start.13
  98.8 1.2 copy-done.13
  100.0 37.3 %gather_part.1 = (bf16[9216,512]{1,0:T(8,128)(2,1)S(1)}, f32[2,128,512]{2,1,0:T(8,128)S(1)}, f32[2,512,128]{2,1,0:T(8,128)S(1)}, f32[512,512]{1,0:T(8,128)S(1)},...) custom-call(bf16[9216,512]{1,0:T(8,128)(2,1)S(1)} %copy-done.1, ...), custom_call_target="tpu_custom_call", output_to_operand_aliasing={{0}: (0, {})} | custom-call | flops 10000000000 | bytes 40000000 | tf_op jit(solution)/shard_map/gather_part/pallas_call | solution.py:641
  137.3 0.0 copy-start.2
  137.3 3.7 %copy-done.2 = bf16[9216,512]{1,0:T(8,128)(2,1)} copy-done((bf16[9216,512]{1,0:T(8,128)(2,1)}, bf16[9216,512]{1,0:T(8,128)(2,1)S(1)}, u32[]{:S(2)}) %copy-start.2) | copy-done | bytes 9437208
  141.0 0.0 copy-start.4
  141.0 3.4 %copy-done.4 = f32[2,512,2048]{2,1,0:T(8,128)} copy-done((f32[2,512,2048]{2,1,0:T(8,128)}, f32[2,512,2048]{2,1,0:T(8,128)S(1)}, u32[]{:S(2)}) %copy-start.4) | copy-done | bytes 8388632
  144.4 0.0 copy-start.6
  144.4 3.4 %copy-done.6 = f32[2,2048,512]{2,1,0:T(8,128)} copy-done((f32[2,2048,512]{2,1,0:T(8,128)}, f32[2,2048,512]{2,1,0:T(8,128)S(1)}, u32[]{:S(2)}) %copy-start.6) | copy-done | bytes 8388632
  147.8 0.0 copy-start.8
  147.8 3.4 %copy-done.8 = f32[2,512,2048]{2,1,0:T(8,128)} copy-done((f32[2,512,2048]{2,1,0:T(8,128)}, f32[2,512,2048]{2,1,0:T(8,128)S(1)}, u32[]{:S(2)}) %copy-start.8) | copy-done | bytes 8388632
  151.2 0.0 copy-start.10
  151.2 3.4 %copy-done.10 = f32[2,2048,512]{2,1,0:T(8,128)} copy-done((f32[2,2048,512]{2,1,0:T(8,128)}, f32[2,2048,512]{2,1,0:T(8,128)S(1)}, u32[]{:S(2)}) %copy-start.10) | copy-done | bytes 8388632
  154.6 0.0 copy-start.15
  154.6 1.0 copy-done.15
  155.5 0.0 copy-start.17
  155.6 1.0 copy-done.17
  156.5 0.0 copy-start.19
  156.5 0.8 copy-done.19
  157.3 0.0 copy-start.21
  157.3 0.8 copy-done.21
  158.1 0.0 copy-start.23
  158.1 0.8 copy-done.23
  158.9 0.0 copy-start.25
  158.9 0.8 copy-done.25
  159.7 0.0 copy-start.3
  159.7 3.7 %copy-done.3 = bf16[9216,512]{1,0:T(8,128)(2,1)S(1)} copy-done((bf16[9216,512]{1,0:T(8,128)(2,1)S(1)}, bf16[9216,512]{1,0:T(8,128)(2,1)}, u32[]{:S(2)}) %copy-start.3) | copy-done | bytes 9437208
  163.4 0.0 copy-start.5
  163.4 3.4 %copy-done.5 = f32[2,512,2048]{2,1,0:T(8,128)S(1)} copy-done((f32[2,512,2048]{2,1,0:T(8,128)S(1)}, f32[2,512,2048]{2,1,0:T(8,128)}, u32[]{:S(2)}) %copy-start.5) | copy-done | bytes 8388632
  166.8 0.0 copy-start.7
  166.8 3.4 %copy-done.7 = f32[2,2048,512]{2,1,0:T(8,128)S(1)} copy-done((f32[2,2048,512]{2,1,0:T(8,128)S(1)}, f32[2,2048,512]{2,1,0:T(8,128)}, u32[]{:S(2)}) %copy-start.7) | copy-done | bytes 8388632
  170.1 0.0 copy-start.9
  170.1 3.4 %copy-done.9 = f32[2,512,2048]{2,1,0:T(8,128)S(1)} copy-done((f32[2,512,2048]{2,1,0:T(8,128)S(1)}, f32[2,512,2048]{2,1,0:T(8,128)}, u32[]{:S(2)}) %copy-start.9) | copy-done | bytes 8388632
  173.5 0.0 copy-start.11
  173.5 3.4 %copy-done.11 = f32[2,2048,512]{2,1,0:T(8,128)S(1)} copy-done((f32[2,2048,512]{2,1,0:T(8,128)S(1)}, f32[2,2048,512]{2,1,0:T(8,128)}, u32[]{:S(2)}) %copy-start.11) | copy-done | bytes 8388632
  176.9 0.0 copy-start.14
  176.9 1.2 copy-done.14
  178.1 0.0 copy-start.16
  178.1 1.2 copy-done.16
  179.3 0.0 copy-start.18
  179.4 1.2 copy-done.18
  180.6 0.0 copy-start.20
  180.6 1.0 copy-done.20
  181.6 0.0 copy-start.22
  181.6 1.0 copy-done.22
  182.7 0.0 copy-start.24
  182.7 1.0 copy-done.24
  183.7 0.0 copy-start.26
  183.7 1.0 copy-done.26
  184.7 23.4 %next_part.1 = (f32[4,1000]{1,0:T(4,128)}, f32[2,128,512]{2,1,0:T(8,128)}, f32[2,512,128]{2,1,0:T(8,128)}, f32[512,512]{1,0:T(8,128)}, f32[2,512,2048]{2,1,0:T(8...) custom-call(f32[1000,512]{1,0:T(8,128)} %bitcast.8, ...), custom_call_target="tpu_custom_call", output_to_operand_aliasing={{13}: (12, {}), {14}: (13, {}), {15}: (14, {}), {16}: (15, ... | custom-call | flops 10000000000 | bytes 50000000 | tf_op jit(solution)/shard_map/next_part/pallas_call | solution.py:663
Async XLA Ops:
  90.5 3.7 %copy-start = (bf16[9216,512]{1,0:T(8,128)(2,1)}, bf16[9216,512]{1,0:T(8,128)(2,1)S(1)}, u32[]{:S(2)}) copy-start(bf16[9216,512]{1,0:T(8,128)(2,1)S(1)} %get-tuple-element.41.in_final) | copy-start | bytes 28311556
  94.2 1.0 copy-start.12
  95.1 3.7 %copy-start.1 = (bf16[9216,512]{1,0:T(8,128)(2,1)S(1)}, bf16[9216,512]{1,0:T(8,128)(2,1)}, u32[]{:S(2)}) copy-start(bf16[9216,512]{1,0:T(8,128)(2,1)} %copy-done) | copy-start | bytes 28311556
  98.8 1.2 copy-start.13
  137.3 3.7 %copy-start.2 = (bf16[9216,512]{1,0:T(8,128)(2,1)}, bf16[9216,512]{1,0:T(8,128)(2,1)S(1)}, u32[]{:S(2)}) copy-start(bf16[9216,512]{1,0:T(8,128)(2,1)S(1)} %get-tuple-element.43.sums) | copy-start | bytes 28311556
  141.0 3.4 %copy-start.4 = (f32[2,512,2048]{2,1,0:T(8,128)}, f32[2,512,2048]{2,1,0:T(8,128)S(1)}, u32[]{:S(2)}) copy-start(f32[2,512,2048]{2,1,0:T(8,128)S(1)} %get-tuple-element.52.in_wu) | copy-start | bytes 25165828
  144.4 3.4 %copy-start.6 = (f32[2,2048,512]{2,1,0:T(8,128)}, f32[2,2048,512]{2,1,0:T(8,128)S(1)}, u32[]{:S(2)}) copy-start(f32[2,2048,512]{2,1,0:T(8,128)S(1)} %get-tuple-element.53.in_wd) | copy-start | bytes 25165828
  147.8 3.4 %copy-start.8 = (f32[2,512,2048]{2,1,0:T(8,128)}, f32[2,512,2048]{2,1,0:T(8,128)S(1)}, u32[]{:S(2)}) copy-start(f32[2,512,2048]{2,1,0:T(8,128)S(1)} %get-tuple-element.54.in_vu) | copy-start | bytes 25165828
  151.2 3.4 %copy-start.10 = (f32[2,2048,512]{2,1,0:T(8,128)}, f32[2,2048,512]{2,1,0:T(8,128)S(1)}, u32[]{:S(2)}) copy-start(f32[2,2048,512]{2,1,0:T(8,128)S(1)} %get-tuple-element.55.in_vd) | copy-start | bytes 25165828
  154.6 1.0 copy-start.15
  155.5 1.0 copy-start.17
  156.5 0.8 copy-start.19
  157.3 0.8 copy-start.21
  158.1 0.8 copy-start.23
  158.9 0.8 copy-start.25
  159.7 3.7 %copy-start.3 = (bf16[9216,512]{1,0:T(8,128)(2,1)S(1)}, bf16[9216,512]{1,0:T(8,128)(2,1)}, u32[]{:S(2)}) copy-start(bf16[9216,512]{1,0:T(8,128)(2,1)} %copy-done.2) | copy-start | bytes 28311556
  163.4 3.4 %copy-start.5 = (f32[2,512,2048]{2,1,0:T(8,128)S(1)}, f32[2,512,2048]{2,1,0:T(8,128)}, u32[]{:S(2)}) copy-start(f32[2,512,2048]{2,1,0:T(8,128)} %copy-done.4) | copy-start | bytes 25165828
  166.8 3.4 %copy-start.7 = (f32[2,2048,512]{2,1,0:T(8,128)S(1)}, f32[2,2048,512]{2,1,0:T(8,128)}, u32[]{:S(2)}) copy-start(f32[2,2048,512]{2,1,0:T(8,128)} %copy-done.6) | copy-start | bytes 25165828
  170.1 3.4 %copy-start.9 = (f32[2,512,2048]{2,1,0:T(8,128)S(1)}, f32[2,512,2048]{2,1,0:T(8,128)}, u32[]{:S(2)}) copy-start(f32[2,512,2048]{2,1,0:T(8,128)} %copy-done.8) | copy-start | bytes 25165828
  173.5 3.4 %copy-start.11 = (f32[2,2048,512]{2,1,0:T(8,128)S(1)}, f32[2,2048,512]{2,1,0:T(8,128)}, u32[]{:S(2)}) copy-start(f32[2,2048,512]{2,1,0:T(8,128)} %copy-done.10) | copy-start | bytes 25165828
  176.9 1.2 copy-start.14
  178.1 1.2 copy-start.16
  179.3 1.2 copy-start.18
  180.6 1.0 copy-start.20
  181.6 1.0 copy-start.22
  182.7 1.0 copy-start.24
  183.7 1.0 copy-start.26

commit v5 on v3

--- a/solution.py
+++ b/solution.py
@@ -89,12 +89,14 @@
 
 def stage_one_forward(r0, r1, r2, up_one, down_one):
     def body(j, carry):
-        sl = lanes(j, WIDTH)
-        mid = stage_one_block(r0[:, sl], up_one[0], down_one[0])
-        r1[:, sl] = mid
-        r2[:, sl] = stage_one_block(mid, up_one[1], down_one[1])
+        cuts = [lanes(2 * j + k, WIDTH) for k in range(2)]
+        mids = [stage_one_block(r0[:, sl], up_one[0], down_one[0]) for sl in cuts]
+        for sl, mid in zip(cuts, mids):
+            r1[:, sl] = mid
+        for sl, mid in zip(cuts, mids):
+            r2[:, sl] = stage_one_block(mid, up_one[1], down_one[1])
         return carry
-    lax.fori_loop(0, 4, body, 0)
+    lax.fori_loop(0, 2, body, 0)
 
 
 def stage_two_block(src, dst, normed_ref, acc, up_ref, down_ref):
@@ -473,7 +475,8 @@
         new_w = w[...] - new_v
         v[...] = new_v
         w[...] = new_w
-        b[...] = new_w.astype(BF16)
+        if b is not None:
+            b[...] = new_w.astype(BF16)
 
     def update(i, carry):
         update_piece(*piece(i))
@@ -495,7 +498,7 @@
         h, part = i // 2, lax.rem(i, 2)
         rows, cols = lanes(part, 256), lanes(h, 256)
         g_rows = pl.ds(pl.multiple_of(h * 512, 512), 256)
-        return w.at[rows, cols], v.at[rows, cols], g.at[g_rows, rows], b.at[rows, cols]
+        return w.at[rows, cols], v.at[rows, cols], g.at[g_rows, rows], b if b is None else b.at[rows, cols]
     return piece
 
 
@@ -504,7 +507,7 @@
         h, part = i // 2, lax.rem(i, 2)
         rows = pl.ds(pl.multiple_of(i * 128, 128), 128)
         g_rows = pl.ds(pl.multiple_of(h * 512 + 256 + part * 128, 128), 128)
-        return w.at[rows], v.at[rows], g.at[g_rows], b.at[rows]
+        return w.at[rows], v.at[rows], g.at[g_rows], b if b is None else b.at[rows]
     return piece
 
 
@@ -554,12 +557,13 @@
     wait_all(head.stores)
     start_all(wide_downs[1].loads)
     stage_one_forward(r0, s0, s1, up1, dn1)
+    wide_ups[1].update(16, up_pieces, sums.at[pl.ds(0, HELD * UNIT)], None)
+    wide_downs[1].update(16, down_pieces, sums.at[pl.ds(0, HELD * UNIT)], None)
     s0[...] = dot_nn(s1[...], mg[...]).astype(BF16)
-    for n, (src, dst) in enumerate(((s0, s1), (s1, s0))):
-        if n:
-            wide_ups[n].update(16, up_pieces, sums.at[pl.ds(0, HELD * UNIT)], up2)
-            wide_downs[n].update(16, down_pieces, sums.at[pl.ds(0, HELD * UNIT)], dn2)
-        stage_two_block(src, dst, normed_ref, acc, up2, dn2)
+    stage_two_block(s0, s1, normed_ref, acc, up2, dn2)
+    cast_rows(up2, wb_up2, WIDE, 16)
+    cast_rows(dn2, wb_dn2, HID_TWO, SHARD)
+    stage_two_block(s1, s0, normed_ref, acc, up2, dn2)
     head_b = pooled_norm(s0[...])[0].astype(BF16)
     logits_ref[...] = dot_nt(head_b, hd[...])[:IMGS]
     for each in ups + downs + [merge] + wide_ups + wide_downs:

time: 157 us -> 156 us (level)
  no operation moved by 1% of the time
where the time goes in v5:
time: 156 us; the launch traced here: 155 us
  Pallas kernels  155 us (99%)
    pallas_call x1, Pallas kernels, run_train(): pl.pallas_call(train_kernel, out_shape=[vmem(*each) for each in HANDED] +...  120 us
    pallas_call x1, Pallas kernels, run_next(): pl.pallas_call(next_kernel, out_shape=f32_outs([(IMGS, CLASSES)] + list(W...  34.4 us

profile of v5, /device:TPU:0, one launch (start us, length us, event | category | flops | bytes accessed | tf_op | source)
XLA Modules:
  0.0 155.4 jit_solution(5582448472372563235)
XLA Ops:
  0.6 120.1 %train_part.1 = (bf16[9216,512]{1,0:T(8,128)(2,1)S(1)}, f32[2,128,512]{2,1,0:T(8,128)S(1)}, f32[2,512,128]{2,1,0:T(8,128)S(1)}, f32[512,512]{1,0:T(8,128)S(1)}, ...) custom-call(bf16[3136,128]{1,0:T(8,128)(2,1)} %bitcast.11, ...), custom_call_target="tpu_custom_call" | custom-call | flops 30000001024 | bytes 40000000 | tf_op jit(solution)/shard_map/train_part/pallas_call | solution.py:601
  120.8 34.4 %next_part.1 = (f32[4,1000]{1,0:T(4,128)}, f32[2,128,512]{2,1,0:T(8,128)}, f32[2,512,128]{2,1,0:T(8,128)}, f32[512,512]{1,0:T(8,128)}, f32[2,512,2048]{2,1,0:T(8...) custom-call(f32[2,512,2048]{2,1,0:T(8,128)} %up2_hbm.3, ...), custom_call_target="tpu_custom_call", output_to_operand_aliasing={{13}: (10, {}), {14}: (11, {}), {15}: (12, {}), {16}: (13, ... | custom-call | flops 10000000000 | bytes 100000000 | tf_op jit(solution)/shard_map/next_part/pallas_call | solution.py:621

commit v6 on v5

--- a/solution.py
+++ b/solution.py
@@ -87,8 +87,10 @@
     return (res_f + dot_nn(act, w_down)).astype(BF16)
 
 
-def stage_one_forward(r0, r1, r2, up_one, down_one):
+def stage_one_forward(r0, r1, r2, up_one, down_one, slots=()):
     def body(j, carry):
+        for k, steps in enumerate(slots):
+            pl.when(j == k)(lambda steps=steps: run_all(steps))
         cuts = [lanes(2 * j + k, WIDTH) for k in range(2)]
         mids = [stage_one_block(r0[:, sl], up_one[0], down_one[0]) for sl in cuts]
         for sl, mid in zip(cuts, mids):
@@ -162,6 +164,11 @@
 
 def total_of(tile):
     return jnp.sum(jnp.sum(tile, axis=0, keepdims=True), axis=1, keepdims=True)
+
+
+def run_all(steps):
+    for action, unit in steps:
+        action(unit)
 
 
 class Links:
@@ -250,11 +257,11 @@
         self.start(unit, phase + 1)
 
 
-def train_kernel(x_hbm, x_next_hbm, labels_ref, up1_hbm, dn1_hbm, mg_hbm, up2_hbm, dn2_hbm, hd_hbm,
-                 final, st_up1, st_dn1, st_mg, st_up2, st_dn2, r0, g_hd, scale_ref,
-                 x_v, x_f32,
+def train_kernel(x_hbm, x_next_hbm, vup1_hbm, vdn1_hbm, vmg_hbm, labels_ref, up1_hbm, dn1_hbm, mg_hbm, up2_hbm, dn2_hbm, hd_hbm,
+                 final, st_up1, st_dn1, st_mg, st_up2, st_dn2, r0, g_hd, x_f32, acc, scale_ref,
+                 x_v, gb_turn,
                  up1, dn1, mg, up2, dn2, hd,
-                 r1, r2, s0, s1, normed_ref, acc, grad_a, grad_b, sems,
+                 r1, r2, s0, s1, normed_ref, grad_a, grad_b, sems,
                  du1, dv1, own, land1, land2, factors, w_sums, g_sums, link_sems, factor_sems):
     links = Links(own, final, land1, land2, link_sems)
     me = links.me
@@ -381,6 +388,26 @@
     reloads = [pltpu.make_async_copy(src, dst, sems.at[9 + i]) for i, (src, dst) in enumerate((
         (up2_hbm.at[0], st_up2), (dn2_hbm.at[1], st_dn2), (x_next_hbm, x_v), (dn2_hbm.at[0], st_dn2)))]
 
+    speeds = [pltpu.make_async_copy(src, dst, sems.at[13 + i]) for i, (src, dst) in enumerate((
+        (vup1_hbm.at[0], acc.at[pl.ds(0, WIDTH)]), (vup1_hbm.at[1], acc.at[pl.ds(WIDTH, WIDTH)]), (vmg_hbm, acc.at[pl.ds(TILE, WIDE)]),
+        (vdn1_hbm.at[0], x_f32.at[pl.ds(0, WIDE)]), (vdn1_hbm.at[1], x_f32.at[pl.ds(WIDE, WIDE)])))]
+
+    def scale_of(matrix):
+        sl = pl.ds(matrix * SUBLANES, SUBLANES)
+        scale = TRUST * (jnp.sqrt(w_sums[sl, :]) / jnp.sqrt(total_of(g_sums[matrix])))
+        scale_ref[sl, :] = scale
+        return scale[:1, :1]
+
+    def update_small(_):
+        wait_all(speeds)
+        small = final.at[pl.ds(LAST * UNIT, UNIT)]
+        for n in range(2):
+            grad = small.at[pl.ds(WIDE + n * WIDTH, WIDTH)]
+            lars_matrix(2, row_pieces(st_up1.at[n], acc.at[pl.ds(n * WIDTH, WIDTH)], grad, up1.at[n], SHARD), scale_of(n))
+            gb_turn[...] = small[pl.ds(WIDE + TILE + n * WIDTH, WIDTH), :].astype(F32).T
+            lars_matrix(4, row_pieces(st_dn1.at[n], x_f32.at[pl.ds(n * WIDE, WIDE)], gb_turn, dn1.at[n], WIDTH), scale_of(2 + n))
+        lars_matrix(8, row_pieces(st_mg, acc.at[pl.ds(TILE, WIDE)], small.at[pl.ds(0, WIDE)], mg, SHARD), scale_of(4))
+
     def weigh_small(_):
         for n in range(2):
             weigh(n, st_up1.at[n], WIDTH, SHARD)
@@ -397,6 +424,7 @@
         weigh(8, st_dn2, HID_TWO, SHARD)
         reloads[3].start()
         permute_tokens(x_v, x_f32, r0)
+        start_all(speeds)
 
     def weigh_second(_):
         reloads[3].wait()
@@ -408,10 +436,6 @@
 
     def back_pair(unit):
         links.forward(unit, FIRST_BACK)
-
-    def run_all(steps):
-        for action, unit in steps:
-            action(unit)
 
     g_sums[...] = jnp.zeros_like(g_sums)
     links.reduce_pair(7)
@@ -460,13 +484,16 @@
     lax.fori_loop(0, half_tiles, head_tile, 0)
     run_all(((links.reduce_pair, LAST), (reduced, 5), (back_first, 3)))
     lax.fori_loop(half_tiles, 2 * half_tiles, head_tile, 0)
-    run_all(((reduced, 6), (weigh_small, 0), (first, LAST), (weigh_first, 0), (back_pair, 0), (back_pair, 1), (finish, 0), (weigh_second, 0), (back_pair, 2), (finish, 1), (reduced, 7),
-             (reduced, LAST), (back_first, 4), (finish, 2), (back_first, 5), (back_pair, 3), (back_first, 6), (back_first, LAST),
-             (finish, 3), (back_pair, 4), (back_first, 7), (back_pair, 5), (finish, 4), (back_pair, LAST), (back_pair, 6), (finish, 5),
-             (finish, LAST), (back_pair, 7), (finish, 6), (finish, 7)))
-    for matrix in range(MATRICES):
-        sl = pl.ds(matrix * SUBLANES, SUBLANES)
-        scale_ref[sl, :] = TRUST * (jnp.sqrt(w_sums[sl, :]) / jnp.sqrt(total_of(g_sums[matrix])))
+    run_all(((reduced, 6), (weigh_small, 0), (first, LAST), (weigh_first, 0), (back_pair, 0), (back_pair, 1), (finish, 0), (reduced, 7),
+             (reduced, LAST), (weigh_second, 0), (back_pair, 2), (finish, 1), (back_first, 4), (finish, 2), (back_first, LAST),
+             (back_first, 5), (back_pair, 3), (back_first, 6), (finish, 3), (back_pair, LAST), (back_pair, 4), (back_first, 7),
+             (finish, LAST), (update_small, 0)))
+    stage_one_forward(r0, r1, r2, up1, dn1, (((back_pair, 5), (finish, 4)), ((back_pair, 6), (finish, 5))))
+    run_all(((back_pair, 7), (finish, 6)))
+    r0[...] = dot_nn(r2[...], mg[...]).astype(BF16)
+    finish(7)
+    for matrix in range(5, MATRICES):
+        scale_of(matrix)
 
 
 def lars_matrix(steps, piece, scale, tails=()):
@@ -525,48 +552,40 @@
         start_all(self.stores)
 
 
-def next_kernel(up2_hbm, dn2_hbm, hd_hbm, vup1_hbm, vdn1_hbm, vmg_hbm, vup2_hbm, vdn2_hbm, vhd_hbm,
-                sums, in_up1, in_dn1, in_mg, in_up2, in_dn2, r0, g_hd, scales,
+def next_kernel(up2_hbm, dn2_hbm, hd_hbm, vup2_hbm, vdn2_hbm, vhd_hbm,
+                sums, w_up1, w_dn1, w_mg, in_up2, in_dn2, mid, g_hd, v_down, v_rest, scales,
                 logits_ref, o_up1, o_dn1, o_mg, o_up2, o_dn2, o_hd, ov_up1, ov_dn1, ov_mg, ov_up2, ov_dn2, ov_hd,
-                w_up1, w_dn1, w_mg, w_up2, w_dn2,
-                vb_up1, vb_dn1, vb_mg, vb_up2, vb_dn2, wb_up2, wb_dn2,
-                gb_turn, up1, dn1, mg, up2, dn2, hd, s0, s1, normed_ref, acc, sems):
-    ups = [Pair(None, vup1_hbm.at[n], o_up1.at[n], ov_up1.at[n], w_up1.at[n], vb_up1.at[n], sems, scales, n) for n in range(2)]
-    downs = [Pair(None, vdn1_hbm.at[n], o_dn1.at[n], ov_dn1.at[n], w_dn1.at[n], vb_dn1.at[n], sems, scales, 2 + n) for n in range(2)]
-    merge = Pair(None, vmg_hbm, o_mg, ov_mg, w_mg, vb_mg, sems, scales, 4)
+                w_up2, w_dn2,
+                vb_up2, vb_dn2, wb_up2, wb_dn2, up2, dn2, hd, s1, normed_ref, acc, sems, small_sems):
+    done = [pltpu.make_async_copy(src, dst, small_sems.at[i]) for i, (src, dst) in enumerate((
+        (w_up1, o_up1), (w_dn1, o_dn1), (w_mg, o_mg), (v_rest.at[pl.ds(TILE, WIDE)], ov_mg),
+        (v_rest.at[pl.ds(0, WIDTH)], ov_up1.at[0]), (v_rest.at[pl.ds(WIDTH, WIDTH)], ov_up1.at[1]),
+        (v_down.at[pl.ds(0, WIDE)], ov_dn1.at[0]), (v_down.at[pl.ds(WIDE, WIDE)], ov_dn1.at[1])))]
     wide_ups = [Pair((None, up2_hbm.at[1])[n], vup2_hbm.at[n], o_up2.at[n], ov_up2.at[n], (w_up2, wb_up2)[n], vb_up2.at[n],
                      sems, scales, 5 + n) for n in range(2)]
     wide_downs = [Pair((None, dn2_hbm.at[1])[n], vdn2_hbm.at[n], o_dn2.at[n], ov_dn2.at[n], (w_dn2, wb_dn2)[n], vb_dn2.at[n],
                        sems, scales, 7 + n) for n in range(2)]
     wb_hd, vb_hd = wb_dn2.at[pl.ds(0, CLASSES)], vb_dn2.at[1, pl.ds(0, CLASSES)]
     head = Pair(hd_hbm, vhd_hbm, o_hd, ov_hd, wb_hd, vb_hd, sems, scales, 9)
-    for each in ups + downs + [merge, head] + wide_ups[:1]:
+    for each in [head] + wide_ups[:1] + wide_downs[:1]:
         start_all(each.loads)
-    small = sums.at[pl.ds(LAST * UNIT, UNIT)]
-    for n in range(2):
-        ups[n].update(2, row_pieces, small.at[pl.ds(WIDE + n * WIDTH, WIDTH)], up1.at[n], SHARD)
-        gb_turn[...] = small[pl.ds(WIDE + TILE + n * WIDTH, WIDTH), :].astype(F32).T
-        downs[n].update(4, row_pieces, gb_turn, dn1.at[n], WIDTH)
-    start_all(wide_downs[0].loads)
-    merge.update(8, row_pieces, small.at[pl.ds(0, WIDE)], mg, SHARD)
+    start_all(done)
+    start_all(wide_ups[1].loads)
     tail = pl.ds(992, SUBLANES)
     head.update(31, row_pieces, g_hd, hd, 32, tails=[(wb_hd.at[tail], vb_hd.at[tail], g_hd.at[tail], hd.at[tail])])
-    start_all(wide_ups[1].loads)
     wide_ups[0].update(16, up_pieces, sums.at[pl.ds(HELD * UNIT, HELD * UNIT)], up2)
     wide_downs[0].update(16, down_pieces, sums.at[pl.ds(HELD * UNIT, HELD * UNIT)], dn2)
     wait_all(head.stores)
     start_all(wide_downs[1].loads)
-    stage_one_forward(r0, s0, s1, up1, dn1)
     wide_ups[1].update(16, up_pieces, sums.at[pl.ds(0, HELD * UNIT)], None)
-    wide_downs[1].update(16, down_pieces, sums.at[pl.ds(0, HELD * UNIT)], None)
-    s0[...] = dot_nn(s1[...], mg[...]).astype(BF16)
-    stage_two_block(s0, s1, normed_ref, acc, up2, dn2)
+    stage_two_block(mid, s1, normed_ref, acc, up2, dn2)
+    wide_downs[1].update(16, down_pieces, sums.at[pl.ds(0, HELD * UNIT)], dn2)
     cast_rows(up2, wb_up2, WIDE, 16)
-    cast_rows(dn2, wb_dn2, HID_TWO, SHARD)
-    stage_two_block(s1, s0, normed_ref, acc, up2, dn2)
-    head_b = pooled_norm(s0[...])[0].astype(BF16)
+    stage_two_block(s1, s1, normed_ref, acc, up2, dn2)
+    head_b = pooled_norm(s1[...])[0].astype(BF16)
     logits_ref[...] = dot_nt(head_b, hd[...])[:IMGS]
-    for each in ups + downs + [merge] + wide_ups + wide_downs:
+    wait_all(done)
+    for each in wide_ups + wide_downs:
         wait_all(each.stores)
 
 
@@ -593,44 +612,45 @@
 DMA = pltpu.SemaphoreType.DMA
 
 
-HANDED = ((SHARE_ROWS, WIDE), BF16), *((shape, F32) for shape in BUF_SHAPES[:5]), ((ROWS, WIDE), BF16), ((CLASS_PAD, WIDE), BF16)
-HANDED_BYTES = 22_000_000
-
-
-def run_train(x_now, x_next, labels, params):
+HANDED = ((SHARE_ROWS, WIDE), BF16), *((shape, F32) for shape in BUF_SHAPES[:5]), ((ROWS, WIDE), BF16), ((CLASS_PAD, WIDE), BF16), \
+    ((ROWS * 4, WIDTH), F32), ((ROWS, WIDE), F32)
+HANDED_BYTES = 25_200_000
+
+
+def run_train(x_now, x_next, labels, params, velocities):
     return pl.pallas_call(
         train_kernel,
         out_shape=[vmem(*each) for each in HANDED] + f32_outs([(MATRICES * SUBLANES, WIDTH)]),
-        in_specs=[ANY_SPEC] * 2 + [pl.BlockSpec(memory_space=pltpu.SMEM)] + [ANY_SPEC] * 6,
-        out_specs=[VMEM_SPEC] * 9,
-        scratch_shapes=[vmem((ROWS * 4, WIDTH), BF16), vmem((ROWS * 4, WIDTH), F32)]
+        in_specs=[ANY_SPEC] * 5 + [pl.BlockSpec(memory_space=pltpu.SMEM)] + [ANY_SPEC] * 6,
+        out_specs=[VMEM_SPEC] * 11,
+        scratch_shapes=[vmem((ROWS * 4, WIDTH), BF16), vmem((WIDE, WIDTH), F32)]
         + [vmem(shape, BF16) for shape in W_SHAPES[:5]] + [vmem((CLASS_PAD, WIDE), BF16)]
-        + [act()] * 5 + [act(F32), act(), act(), DMA((13,)), vmem((WIDTH, WIDE), F32), vmem((WIDTH, WIDE), F32)]
+        + [act()] * 7 + [DMA((18,)), vmem((WIDTH, WIDE), F32), vmem((WIDTH, WIDE), F32)]
         + [vmem((rows, WIDE), BF16) for rows in (SHARE_ROWS, N_UNITS * TILE, N_UNITS * WIDTH)]
         + [vmem((DEVS, SUBLANES, WIDE + CLASS_PAD), BF16), vmem((MATRICES * SUBLANES, WIDTH), F32), vmem((MATRICES, SUBLANES, WIDE), F32)]
         + [DMA((N_UNITS, 6, 2, 2)), DMA((DEVS, 2))],
         compiler_params=pltpu.CompilerParams(vmem_limit_bytes=VMEM_BYTES - HANDED_BYTES, collective_id=0, has_side_effects=True),
         cost_estimate=pl.CostEstimate(flops=30_000_000_000, bytes_accessed=40_000_000, transcendentals=0),
         name='train_part',
-    )(x_now, x_next, labels, *params)
+    )(x_now, x_next, *velocities[:3], labels, *params)
 
 
 def run_next(params, velocities, handed):
-    held = [vmem(*each) for each in HANDED[1:6]]
-    handed = [pltpu.with_memory_space_constraint(each, pltpu.VMEM) for each in handed[:8]] + list(handed[8:])
+    held = [vmem(*each) for each in HANDED[4:6]]
+    handed = [pltpu.with_memory_space_constraint(each, pltpu.VMEM) for each in handed[:10]] + list(handed[10:])
     outs = pl.pallas_call(
         next_kernel,
         out_shape=f32_outs([(IMGS, CLASSES)] + list(W_SHAPES) * 2) + held,
-        in_specs=[ANY_SPEC] * 9 + [VMEM_SPEC] * 9,
-        out_specs=[VMEM_SPEC] + [ANY_SPEC] * 12 + [VMEM_SPEC] * 5,
-        scratch_shapes=[vmem(shape, F32) for shape in W_SHAPES[:5] + BUF_SHAPES[3:5]] + [vmem((WIDE, WIDTH), F32)]
-        + [vmem(shape, BF16) for shape in BUF_SHAPES]
-        + [act()] * 3 + [act(F32), DMA((10, 2, 2))],
-        input_output_aliases={10 + i: 13 + i for i in range(5)},
+        in_specs=[ANY_SPEC] * 6 + [VMEM_SPEC] * 11,
+        out_specs=[VMEM_SPEC] + [ANY_SPEC] * 12 + [VMEM_SPEC] * 2,
+        scratch_shapes=[vmem(shape, F32) for shape in W_SHAPES[3:5] + BUF_SHAPES[3:5]]
+        + [vmem(shape, BF16) for shape in BUF_SHAPES[3:]]
+        + [act()] * 2 + [act(F32), DMA((10, 2, 2)), DMA((8,))],
+        input_output_aliases={10 + i: 13 + i for i in range(2)},
         compiler_params=pltpu.CompilerParams(vmem_limit_bytes=VMEM_BYTES - HANDED_BYTES),
         cost_estimate=pl.CostEstimate(flops=10_000_000_000, bytes_accessed=100_000_000, transcendentals=0),
         name='next_part',
-    )(*params[3:], *velocities, *handed)
+    )(*params[3:], *velocities[3:], *handed)
     return outs[:13]
 
 
@@ -641,7 +661,7 @@
 def solution(mesh):
     def local_step(x_now, labels_now, x_next, *weights):
         params, velocities = turn_head(weights[:6]), turn_head(weights[6:])
-        handed = run_train(x_now.reshape(ROWS * 4, WIDTH), x_next.reshape(ROWS * 4, WIDTH), labels_now, params)
+        handed = run_train(x_now.reshape(ROWS * 4, WIDTH), x_next.reshape(ROWS * 4, WIDTH), labels_now, params, velocities)
         outs = run_next(params, velocities, handed)
         return (outs[0], *turn_head(outs[1:7]), *turn_head(outs[7:]))
 

time: 156 us -> 155 us (level)
    pallas_call x1, Pallas kernels: 34.4 us -> 31 us  [run_next(): pl.pallas_call(next_kernel, out_shape=f32_outs([(IMGS, CLASSES)] + list(W...]
    pallas_call x1, Pallas kernels: 120 us -> 123 us  [run_train(): pl.pallas_call(train_kernel, out_shape=[vmem(*each) for each in HANDED] +...]
where the time goes in v6:
time: 155 us
  Pallas kernels  154 us (99%)
    pallas_call x1, Pallas kernels, run_train(): pl.pallas_call(train_kernel, out_shape=[vmem(*each) for each in HANDED] +...  123 us
    pallas_call x1, Pallas kernels, run_next(): pl.pallas_call(next_kernel, out_shape=f32_outs([(IMGS, CLASSES)] + list(W...  31 us

profile of v6, /device:TPU:0, one launch (start us, length us, event | category | flops | bytes accessed | tf_op | source)
XLA Modules:
  0.0 155.3 jit_solution(2415581660000444624)
XLA Ops:
  0.6 123.4 %train_part.1 = (bf16[9216,512]{1,0:T(8,128)(2,1)S(1)}, f32[2,128,512]{2,1,0:T(8,128)S(1)}, f32[2,512,128]{2,1,0:T(8,128)S(1)}, f32[512,512]{1,0:T(8,128)S(1)}, ...) custom-call(bf16[3136,128]{1,0:T(8,128)(2,1)} %bitcast.11, ...), custom_call_target="tpu_custom_call" | custom-call | flops 30000001024 | bytes 40000000 | tf_op jit(solution)/shard_map/train_part/pallas_call | solution.py:621
  124.1 31.0 %next_part.1 = (f32[4,1000]{1,0:T(4,128)}, f32[2,128,512]{2,1,0:T(8,128)}, f32[2,512,128]{2,1,0:T(8,128)}, f32[512,512]{1,0:T(8,128)}, f32[2,512,2048]{2,1,0:T(8...) custom-call(f32[2,512,2048]{2,1,0:T(8,128)} %up2_hbm.3, ...), custom_call_target="tpu_custom_call", output_to_operand_aliasing={{13}: (10, {}), {14}: (11, {})} | custom-call | flops 10000000000 | bytes 100000000 | tf_op jit(solution)/shard_map/next_part/pallas_call | solution.py:641

commit v7 on v6

--- a/solution.py
+++ b/solution.py
@@ -87,18 +87,18 @@
     return (res_f + dot_nn(act, w_down)).astype(BF16)
 
 
-def stage_one_forward(r0, r1, r2, up_one, down_one, slots=()):
+def stage_one_forward(r0, r1, r2, up_one, down_one, slots=(), group=2):
     def body(j, carry):
         for k, steps in enumerate(slots):
             pl.when(j == k)(lambda steps=steps: run_all(steps))
-        cuts = [lanes(2 * j + k, WIDTH) for k in range(2)]
+        cuts = [lanes(group * j + k, WIDTH) for k in range(group)]
         mids = [stage_one_block(r0[:, sl], up_one[0], down_one[0]) for sl in cuts]
         for sl, mid in zip(cuts, mids):
             r1[:, sl] = mid
         for sl, mid in zip(cuts, mids):
             r2[:, sl] = stage_one_block(mid, up_one[1], down_one[1])
         return carry
-    lax.fori_loop(0, 2, body, 0)
+    lax.fori_loop(0, IMGS // group, body, 0)
 
 
 def stage_two_block(src, dst, normed_ref, acc, up_ref, down_ref):
@@ -488,15 +488,15 @@
              (reduced, LAST), (weigh_second, 0), (back_pair, 2), (finish, 1), (back_first, 4), (finish, 2), (back_first, LAST),
              (back_first, 5), (back_pair, 3), (back_first, 6), (finish, 3), (back_pair, LAST), (back_pair, 4), (back_first, 7),
              (finish, LAST), (update_small, 0)))
-    stage_one_forward(r0, r1, r2, up1, dn1, (((back_pair, 5), (finish, 4)), ((back_pair, 6), (finish, 5))))
-    run_all(((back_pair, 7), (finish, 6)))
+    slots = ((back_pair, 5),), ((back_pair, 6), (finish, 4)), ((finish, 5),), ((back_pair, 7), (finish, 6))
+    stage_one_forward(r0, r1, r2, up1, dn1, slots, 1)
     r0[...] = dot_nn(r2[...], mg[...]).astype(BF16)
     finish(7)
     for matrix in range(5, MATRICES):
         scale_of(matrix)
 
 
-def lars_matrix(steps, piece, scale, tails=()):
+def lars_matrix(steps, piece, scale, tails=(), begin=0):
     def update_piece(w, v, g, b):
         new_v = MOMENTUM * v[...] + scale * g[...].astype(F32)
         new_w = w[...] - new_v
@@ -508,7 +508,7 @@
     def update(i, carry):
         update_piece(*piece(i))
         return carry
-    lax.fori_loop(0, steps, update, 0)
+    lax.fori_loop(begin, begin + steps, update, 0)
     for tail in tails:
         update_piece(*tail)
 
@@ -522,7 +522,7 @@
 
 def up_pieces(w, v, g, b):
     def piece(i):
-        h, part = i // 2, lax.rem(i, 2)
+        part, h = i // N_TILES, lax.rem(i, N_TILES)
         rows, cols = lanes(part, 256), lanes(h, 256)
         g_rows = pl.ds(pl.multiple_of(h * 512, 512), 256)
         return w.at[rows, cols], v.at[rows, cols], g.at[g_rows, rows], b if b is None else b.at[rows, cols]
@@ -539,17 +539,23 @@
 
 
 class Pair:
-    def __init__(self, w, v, out_w, out_v, buf_w, buf_v, sems, scales, slot):
+    def __init__(self, w, v, out_w, out_v, buf_w, buf_v, sems, scales, slot, parts=1):
         self.buf_w, self.buf_v = buf_w, buf_v
         self.scale = scales.at[pl.ds(slot * SUBLANES, 1), pl.ds(0, 1)]
         ins = ((v, buf_v),) if w is None else ((v, buf_v), (w, buf_w))
-        self.loads, self.stores = ([pltpu.make_async_copy(src, dst, sems.at[slot, k, i]) for i, (src, dst) in enumerate(part)]
-                                   for k, part in enumerate((ins, ((buf_w, out_w), (buf_v, out_v)))))
+        self.loads = [pltpu.make_async_copy(src, dst, sems.at[slot, parts, i]) for i, (src, dst) in enumerate(ins)]
+        size = buf_w.shape[0] // parts
+        cuts = [pl.ds(k * size, size) for k in range(parts)]
+        self.parts = [[pltpu.make_async_copy(src.at[sl], dst.at[sl], sems.at[slot, k, i])
+                       for i, (src, dst) in enumerate(((buf_w, out_w), (buf_v, out_v)))] for k, sl in enumerate(cuts)]
+        self.stores = sum(self.parts, [])
 
     def update(self, steps, make, grad, cast, *rest, tails=()):
         wait_all(self.loads)
-        lars_matrix(steps, make(self.buf_w, self.buf_v, grad, cast, *rest), self.scale[...], tails)
-        start_all(self.stores)
+        count = len(self.parts)
+        for k, part in enumerate(self.parts):
+            lars_matrix(steps // count, make(self.buf_w, self.buf_v, grad, cast, *rest), self.scale[...], tails, k * (steps // count))
+            start_all(part)
 
 
 def next_kernel(up2_hbm, dn2_hbm, hd_hbm, vup2_hbm, vdn2_hbm, vhd_hbm,
@@ -562,9 +568,9 @@
         (v_rest.at[pl.ds(0, WIDTH)], ov_up1.at[0]), (v_rest.at[pl.ds(WIDTH, WIDTH)], ov_up1.at[1]),
         (v_down.at[pl.ds(0, WIDE)], ov_dn1.at[0]), (v_down.at[pl.ds(WIDE, WIDE)], ov_dn1.at[1])))]
     wide_ups = [Pair((None, up2_hbm.at[1])[n], vup2_hbm.at[n], o_up2.at[n], ov_up2.at[n], (w_up2, wb_up2)[n], vb_up2.at[n],
-                     sems, scales, 5 + n) for n in range(2)]
+                     sems, scales, 5 + n, 2) for n in range(2)]
     wide_downs = [Pair((None, dn2_hbm.at[1])[n], vdn2_hbm.at[n], o_dn2.at[n], ov_dn2.at[n], (w_dn2, wb_dn2)[n], vb_dn2.at[n],
-                       sems, scales, 7 + n) for n in range(2)]
+                       sems, scales, 7 + n, 4) for n in range(2)]
     wb_hd, vb_hd = wb_dn2.at[pl.ds(0, CLASSES)], vb_dn2.at[1, pl.ds(0, CLASSES)]
     head = Pair(hd_hbm, vhd_hbm, o_hd, ov_hd, wb_hd, vb_hd, sems, scales, 9)
     for each in [head] + wide_ups[:1] + wide_downs[:1]:
@@ -645,7 +651,7 @@
         out_specs=[VMEM_SPEC] + [ANY_SPEC] * 12 + [VMEM_SPEC] * 2,
         scratch_shapes=[vmem(shape, F32) for shape in W_SHAPES[3:5] + BUF_SHAPES[3:5]]
         + [vmem(shape, BF16) for shape in BUF_SHAPES[3:]]
-        + [act()] * 2 + [act(F32), DMA((10, 2, 2)), DMA((8,))],
+        + [act()] * 2 + [act(F32), DMA((10, 5, 2)), DMA((8,))],
         input_output_aliases={10 + i: 13 + i for i in range(2)},
         compiler_params=pltpu.CompilerParams(vmem_limit_bytes=VMEM_BYTES - HANDED_BYTES),
         cost_estimate=pl.CostEstimate(flops=10_000_000_000, bytes_accessed=100_000_000, transcendentals=0),

time: 155 us -> 156 us (level)
  no operation moved by 1% of the time
where the time goes in v7:
time: 156 us
  Pallas kernels  155 us (99%)
    pallas_call x1, Pallas kernels, run_train(): pl.pallas_call(train_kernel, out_shape=[vmem(*each) for each in HANDED] +...  124 us
    pallas_call x1, Pallas kernels, run_next(): pl.pallas_call(next_kernel, out_shape=f32_outs([(IMGS, CLASSES)] + list(W...  31.5 us

profile of v7, /device:TPU:0, one launch (start us, length us, event | category | flops | bytes accessed | tf_op | source)
XLA Modules:
  0.0 156.3 jit_solution(6459934411396016274)
XLA Ops:
  0.6 123.9 %train_part.1 = (bf16[9216,512]{1,0:T(8,128)(2,1)S(1)}, f32[2,128,512]{2,1,0:T(8,128)S(1)}, f32[2,512,128]{2,1,0:T(8,128)S(1)}, f32[512,512]{1,0:T(8,128)S(1)}, ...) custom-call(bf16[3136,128]{1,0:T(8,128)(2,1)} %bitcast.11, ...), custom_call_target="tpu_custom_call" | custom-call | flops 30000001024 | bytes 40000000 | tf_op jit(solution)/shard_map/train_part/pallas_call | solution.py:627
  124.6 31.5 %next_part.1 = (f32[4,1000]{1,0:T(4,128)}, f32[2,128,512]{2,1,0:T(8,128)}, f32[2,512,128]{2,1,0:T(8,128)}, f32[512,512]{1,0:T(8,128)}, f32[2,512,2048]{2,1,0:T(8...) custom-call(f32[2,512,2048]{2,1,0:T(8,128)} %up2_hbm.3, ...), custom_call_target="tpu_custom_call", output_to_operand_aliasing={{13}: (10, {}), {14}: (11, {})} | custom-call | flops 10000000000 | bytes 100000000 | tf_op jit(solution)/shard_map/next_part/pallas_call | solution.py:647
